TPU v7x, 256 devices: a whole 4x4x8 slice. The times are simulated.
256 devices in a mesh: gx: 8 (over z), gy: 8 (over y, core), gz: 4 (over x).
Axes of the slice: x: 4, y: 4, z: 8, core: 2. Of those that a mesh axis runs over, the one named last changes fastest.
Arguments:
- acts: bfloat16 [150528, 2048], P(('gx', 'gy', 'gz')), may hold values from -24 to 24
- saved_hidden: bfloat16 [150528, 512], P(('gx', 'gy', 'gz')), as said below
- grad_out: bfloat16 [150528, 2048], P(('gx', 'gy', 'gz')), may hold values from -24 to 24
- master_reduce: float32 [2048, 512], P(('gx', 'gy', 'gz')), may hold values from -60 to 60
- master_expand: float32 [2048, 512], P(('gx', 'gy', 'gz')), may hold values from -60 to 60
- velocity_reduce: float32 [2048, 512], P(('gx', 'gy', 'gz')), may hold values from -6 to 6
- velocity_expand: float32 [2048, 512], P(('gx', 'gy', 'gz')), may hold values from -6 to 6
Outputs:
- grad_in: bfloat16 [150528, 2048], P(('gx', 'gy', 'gz'))
- new_master_reduce: float32 [2048, 512], P(('gx', 'gy', 'gz'))
- new_master_expand: float32 [2048, 512], P(('gx', 'gy', 'gz'))
- new_velocity_reduce: float32 [2048, 512], P(('gx', 'gy', 'gz'))
- new_velocity_expand: float32 [2048, 512], P(('gx', 'gy', 'gz'))
- work_reduce: bfloat16 [2048, 512], replicated
- work_expand: bfloat16 [2048, 512], replicated
Inputs may be any that keep to these rules, and one draw needn't show every extreme that they name: `saved_hidden`: values are zero or positive, zero at about half of the entries.
All inputs are finite; a program needn't handle non-finite values.
Results may differ from a plain program's by a relative error of at most 0.0064.
Values may be sent and summed in bfloat16 or wider, within the bound.
A program may use at most 64 MiB of HBM per device.

v0:
```python
import jax
import jax.numpy as jnp
from jax import lax
from jax.sharding import Mesh
from jax.sharding import PartitionSpec as P

GX_GY_GZ = ("gx", "gy_0", "gy_1", "gz")


def from_everyone(array, axis):
    peers = lax.axis_size(axis)
    return lax.all_to_all(
        jnp.broadcast_to(array[None], (peers, *array.shape)), axis, 0, 0, tiled=True
    )


def laid_out(parts, dim):
    parts = jnp.moveaxis(parts, 0, dim)
    lengths = parts.shape
    return parts.reshape(*lengths[:dim], lengths[dim] * lengths[dim + 1], *lengths[dim + 2 :])


def whole_of(array, axes, dim):
    far, near = axes
    parts = from_everyone(from_everyone(array, far), near)
    return laid_out(parts.swapaxes(0, 1).reshape(-1, *array.shape), dim)


def split_up(array, dim, peers):
    lengths = array.shape
    parts = array.reshape(*lengths[:dim], peers, lengths[dim] // peers, *lengths[dim + 1 :])
    return jnp.moveaxis(parts, dim, 0)


def summed_on_arrival(array, axis, dim):
    peers = lax.axis_size(axis)
    parts = lax.all_to_all(split_up(array, dim, peers), axis, 0, 0, tiled=True)
    return jnp.sum(parts.astype(jnp.float32), axis=0)


def summed_rows(array, axes, dim):
    far, near = axes
    parts = split_up(array, dim, lax.axis_size(far))
    nearer = summed_on_arrival(parts, near, dim + 1)
    arrived = lax.all_to_all(
        nearer.astype(jnp.bfloat16), far, split_axis=0, concat_axis=0, tiled=True
    )
    return arrived.astype(jnp.float32).sum(axis=0)


def taken_together(array, axis):
    return from_everyone(array, axis).sum(axis=0)


def one_axis_at_a_time(array, axes):
    far, near = axes
    return taken_together(taken_together(array, near), far)


def packed_total(arrays, axis):
    flat, at, outs = (jnp.concatenate([a.reshape(-1) for a in arrays]), 0, [])
    so_far = one_axis_at_a_time(flat, axis)
    for a in arrays:
        outs.append(so_far[at : at + a.size].reshape(a.shape))
        at += a.size
    return tuple(outs)


def sent_together(arrays, axis, dim, along):
    ends, at = ([], 0)
    for a in arrays[:-1]:
        at += a.shape[along]
        ends.append(at)
    both = jnp.concatenate(arrays, axis=along)
    return tuple(jnp.split(lax.all_gather(both, axis, axis=dim, tiled=True), ends, axis=along))


def layer_update(master, grads, velocity, wsquare, gsquare):
    wnorm = jnp.sqrt(wsquare)
    gnorm = jnp.sqrt(gsquare)
    trust = wnorm / (gnorm + 5e-05 * wnorm)
    new_velocity = 0.9 * velocity + trust * (grads + 5e-05 * master)
    new_master = master - 0.1 * new_velocity
    return (new_master, new_velocity)


def shards(
    acts, saved_hidden, grad_out, master_reduce, master_expand, velocity_reduce, velocity_expand
):
    channels = grad_out.shape[1]
    middle = saved_hidden.shape[1]
    inv_c = 1.0 / float(channels) ** 0.5
    inv_m = 1.0 / float(middle) ** 0.5
    cur_reduce = master_reduce.astype(jnp.bfloat16)
    cur_expand = master_expand.astype(jnp.bfloat16)
    columns = grad_out
    summed = jnp.dot(
        columns,
        whole_of(cur_expand, (("gx", "gy_0"), ("gy_1", "gz")), 0),
        preferred_element_type=jnp.float32,
    )
    grad_hidden = jnp.where(saved_hidden > 0, summed * inv_m, 0.0).astype(jnp.bfloat16)
    columns = grad_out
    g_expand = summed_rows(
        (
            lax.dot_general(
                columns, saved_hidden, (((0,), (0,)), ((), ())), preferred_element_type=jnp.float32
            )
            * inv_m
        ).astype(jnp.bfloat16),
        (("gx", "gy_0"), ("gy_1", "gz")),
        0,
    )
    expand_parts = (jnp.sum(master_expand * master_expand), jnp.sum(g_expand * g_expand))
    columns = acts
    g_reduce = summed_rows(
        (
            lax.dot_general(
                columns, grad_hidden, (((0,), (0,)), ((), ())), preferred_element_type=jnp.float32
            )
            * inv_c
        ).astype(jnp.bfloat16),
        (("gx", "gy_0"), ("gy_1", "gz")),
        0,
    )
    back = lax.dot_general(
        grad_hidden,
        whole_of(cur_reduce, (("gx", "gy_0"), ("gy_1", "gz")), 0),
        (((1,), (1,)), ((), ())),
        preferred_element_type=jnp.float32,
    )
    grad_in = (grad_out.astype(jnp.float32) + back * inv_c).astype(jnp.bfloat16)
    reduce_parts = (jnp.sum(master_reduce * master_reduce), jnp.sum(g_reduce * g_reduce))
    totals = packed_total(
        (expand_parts[0], expand_parts[1], reduce_parts[0], reduce_parts[1]),
        (("gx", "gy_0"), ("gy_1", "gz")),
    )
    expand_stats = (totals[0], totals[1])
    reduce_stats = (totals[2], totals[3])
    new_mr, new_vr = layer_update(
        master_reduce, g_reduce, velocity_reduce, reduce_stats[0], reduce_stats[1]
    )
    new_me, new_ve = layer_update(
        master_expand, g_expand, velocity_expand, expand_stats[0], expand_stats[1]
    )
    work_reduce, work_expand = sent_together(
        (new_mr.astype(jnp.bfloat16), new_me.astype(jnp.bfloat16)), GX_GY_GZ, 0, 1
    )
    return (grad_in, new_mr, new_me, new_vr, new_ve, work_reduce, work_expand)


def solution(mesh):
    finer = Mesh(
        mesh.devices.reshape(mesh.shape["gx"], 4, 2, mesh.shape["gz"]), ("gx", "gy_0", "gy_1", "gz")
    )
    return jax.shard_map(
        shards,
        mesh=finer,
        in_specs=(
            P(GX_GY_GZ, None),
            P(GX_GY_GZ, None),
            P(GX_GY_GZ, None),
            P(GX_GY_GZ, None),
            P(GX_GY_GZ, None),
            P(GX_GY_GZ, None),
            P(GX_GY_GZ, None),
        ),
        out_specs=(
            P(GX_GY_GZ, None),
            P(GX_GY_GZ, None),
            P(GX_GY_GZ, None),
            P(GX_GY_GZ, None),
            P(GX_GY_GZ, None),
            P(),
            P(),
        ),
        check_vma=False,
    )
```

profile of v0, /device:TPU:1, one launch (start us, length us, event | category | flops | bytes accessed | tf_op | source)
XLA Modules:
  0.0 311.4 jit_solution(2188358932130534118)
XLA Ops:
  7.2 0.0 copy-start
  7.2 1.5 multiply_reduce_fusion.3
  8.7 23.1 %all_to_all.52 = bf16[32,8,512]{2,1,0:T(8,128)(2,1)S(1)} all-to-all(bf16[32,8,512]{2,1,0:T(8,128)(2,1)S(1)} %broadcast_in_dim.16), channel_id=1, replica_groups=mesh['gx'=8,'gy_0'=4,'gy_1'=2,'gz'=4] {'gx','gy_0'}, dimensions={0} | all-to-all | bytes 524288 | tf_op jit(solution)/shard_map/all_to_all | solution.py:12
  31.8 1.5 broadcast_in_dim.17
  33.3 0.0 copy-start.7
  33.3 6.9 %all-to-all-start.1 = ((bf16[8,32,8,512]{3,2,1,0:T(8,128)(2,1)}), bf16[8,32,8,512]{3,2,1,0:T(8,128)(2,1)}, u32[]{:S(2)}, u32[]{:S(2)}) async-start(bf16[8,32,8,512]{3,2,1,0:T(8,128)(2,1)} %broadcast_in_dim.17), calls=%async_computation.1 | async-start | bytes 4194304 | tf_op jit(solution)/shard_map/all_to_all | solution.py:12
  40.2 0.0 copy-done.7
  40.2 3.5 %multiply_convert_fusion.1 = bf16[2048,512]{1,0:T(8,128)(2,1)S(1)} fusion(bf16[588,2048]{1,0:T(8,128)(2,1)} %param.9, bf16[588,512]{1,0:T(8,128)(2,1)S(1)} %copy-done.7), kind=kOutput, calls=%fused_computation.2 | convolution fusion | flops 1235222528 | bytes 5107712 | tf_op jit(solution)/shard_map/dot_general | solution.py:106
  43.7 1.5 copy.39
  45.3 21.2 %all-to-all-done.1 = bf16[8,32,8,512]{3,2,1,0:T(8,128)(2,1)} async-done(((bf16[8,32,8,512]{3,2,1,0:T(8,128)(2,1)}), bf16[8,32,8,512]{3,2,1,0:T(8,128)(2,1)}, u32[]{:S(2)}, u32[]{:S(2)}) %all-to-all-start.1) | async-done | bytes 2097184 | tf_op jit(solution)/shard_map/all_to_all | solution.py:12
  66.5 4.5 %all-to-all-start.4 = ((bf16[8,32,8,512]{3,2,1,0:T(8,128)(2,1)}), bf16[8,32,8,512]{3,2,1,0:T(8,128)(2,1)}, u32[]{:S(2)}, u32[]{:S(2)}) async-start(bf16[8,32,8,512]{3,2,1,0:T(8,128)(2,1)} %bitcast.31), calls=%async_computation.4 | async-start | bytes 4194304 | tf_op jit(solution)/shard_map/all_to_all | solution.py:37
  71.0 0.0 copy-start.5
  71.0 2.0 copy.25
  73.1 0.3 copy-done.5
  73.4 1.4 fusion.2
  74.8 0.0 copy-start.8
  74.8 0.8 copy-done.8
  75.6 0.0 copy-done
  75.6 3.1 %fusion = bf16[2048,512]{0,1:T(8,128)(2,1)} fusion(bf16[588,512]{1,0:T(8,128)(2,1)S(1)} %fusion.2, bf16[588,2048]{1,0:T(8,128)(2,1)S(1)} %copy-done), kind=kOutput, calls=%fused_computation.3 | convolution fusion | flops 1235222528 | bytes 5107712 | tf_op jit(solution)/shard_map/dot_general | solution.py:118
  78.8 3.9 %copy.28 = bf16[2048,512]{1,0:T(8,128)(2,1)} copy(bf16[2048,512]{0,1:T(8,128)(2,1)} %fusion) | data formatting | bytes 4194304 | tf_op jit(solution)/shard_map/convert_element_type | solution.py:122
  82.7 3.1 copy.29
  85.8 11.5 %all-to-all-done.4 = bf16[8,32,8,512]{3,2,1,0:T(8,128)(2,1)} async-done(((bf16[8,32,8,512]{3,2,1,0:T(8,128)(2,1)}), bf16[8,32,8,512]{3,2,1,0:T(8,128)(2,1)}, u32[]{:S(2)}, u32[]{:S(2)}) %all-to-all-start.4) | async-done | bytes 2097184 | tf_op jit(solution)/shard_map/all_to_all | solution.py:37
  97.4 4.6 %all-to-all-start.6 = ((bf16[8,32,8,512]{3,2,1,0:T(8,128)(2,1)}), bf16[8,32,8,512]{3,2,1,0:T(8,128)(2,1)}, u32[]{:S(2)}, u32[]{:S(2)}) async-start(bf16[8,32,8,512]{3,2,1,0:T(8,128)(2,1)} %copy.29), calls=%async_computation.6 | async-start | bytes 4194304 | tf_op jit(solution)/shard_map/all_to_all | solution.py:37
  101.9 2.7 reduce_sum.97
  104.6 0.0 copy-start.2
  104.6 0.0 copy-start.1
  104.6 0.0 copy-start.3
  104.6 0.0 copy-start.4
  104.6 23.6 %all-to-all-done.6 = bf16[8,32,8,512]{3,2,1,0:T(8,128)(2,1)} async-done(((bf16[8,32,8,512]{3,2,1,0:T(8,128)(2,1)}), bf16[8,32,8,512]{3,2,1,0:T(8,128)(2,1)}, u32[]{:S(2)}, u32[]{:S(2)}) %all-to-all-start.6) | async-done | bytes 2097184 | tf_op jit(solution)/shard_map/all_to_all | solution.py:37
  128.2 3.9 %all-to-all-start.5 = ((bf16[32,8,512]{2,1,0:T(8,128)(2,1)}), bf16[32,8,512]{2,1,0:T(8,128)(2,1)S(1)}, u32[]{:S(2)}, u32[]{:S(2)}) async-start(bf16[32,8,512]{2,1,0:T(8,128)(2,1)} %reduce_sum.97), calls=%async_computation.5 | async-start | bytes 524288 | tf_op jit(solution)/shard_map/all_to_all | solution.py:45
  132.1 2.7 reduce_sum.101
  134.8 9.1 %all-to-all-done.5 = bf16[32,8,512]{2,1,0:T(8,128)(2,1)S(1)} async-done(((bf16[32,8,512]{2,1,0:T(8,128)(2,1)}), bf16[32,8,512]{2,1,0:T(8,128)(2,1)S(1)}, u32[]{:S(2)}, u32[]{:S(2)}) %all-to-all-start.5) | async-done | bytes 262176 | tf_op jit(solution)/shard_map/all_to_all | solution.py:45
  143.8 4.4 %all-to-all-start.7 = ((bf16[32,8,512]{2,1,0:T(8,128)(2,1)}), bf16[32,8,512]{2,1,0:T(8,128)(2,1)S(1)}, u32[]{:S(2)}, u32[]{:S(2)}) async-start(bf16[32,8,512]{2,1,0:T(8,128)(2,1)} %reduce_sum.101), calls=%async_computation.7 | async-start | bytes 524288 | tf_op jit(solution)/shard_map/all_to_all | solution.py:45
  148.2 0.0 all-gather.2.cloned.1.call-start
  148.3 0.0 copy-done.2
  148.3 0.6 multiply_reduce_fusion.1
  148.9 0.6 multiply_reduce_fusion.2
  149.5 9.1 %all-to-all-done.7 = bf16[32,8,512]{2,1,0:T(8,128)(2,1)S(1)} async-done(((bf16[32,8,512]{2,1,0:T(8,128)(2,1)}), bf16[32,8,512]{2,1,0:T(8,128)(2,1)S(1)}, u32[]{:S(2)}, u32[]{:S(2)}) %all-to-all-start.7) | async-done | bytes 262176 | tf_op jit(solution)/shard_map/all_to_all | solution.py:45
  158.7 0.6 multiply_reduce_fusion
  159.3 2.7 pad_maximum_fusion.1
  162.0 10.5 %all_to_all.53 = f32[8,1,4]{2,1,0:T(1,128)S(1)} all-to-all(f32[8,1,4]{2,1,0:T(1,128)S(1)} %broadcast_in_dim.21), channel_id=1, replica_groups=mesh['gx'=8,'gy_0'=4,'gy_1'=2,'gz'=4] {'gy_1','gz'}, dimensions={0} | all-to-all | bytes 256 | tf_op jit(solution)/shard_map/all_to_all | solution.py:12
  172.5 11.9 %all_to_all.54 = f32[32,1,4]{2,1,0:T(1,128)S(1)} all-to-all(f32[32,1,4]{2,1,0:T(1,128)S(1)} %broadcast_in_dim.22), channel_id=1, replica_groups=mesh['gx'=8,'gy_0'=4,'gy_1'=2,'gz'=4] {'gx','gy_0'}, dimensions={0} | all-to-all | bytes 1024 | tf_op jit(solution)/shard_map/all_to_all | solution.py:12
  184.4 0.1 reduce_sum.105
  184.4 0.6 fusion.6
  187.9 0.0 copy-done.1
  187.9 0.0 copy-done.3
  187.9 0.6 fusion.4
  188.5 0.0 copy-done.4
  188.5 0.6 fusion.3
  189.1 0.6 pad_maximum_fusion
  189.7 0.0 all-gather.2.cloned.1.call-update
  189.8 13.6 %all_to_all.55 = bf16[32,8,512]{2,1,0:T(8,128)(2,1)S(1)} all-to-all(bf16[32,8,512]{2,1,0:T(8,128)(2,1)S(1)} %broadcast_in_dim.19), channel_id=1, replica_groups=mesh['gx'=8,'gy_0'=4,'gy_1'=2,'gz'=4] {'gx','gy_0'}, dimensions={0} | all-to-all | bytes 524288 | tf_op jit(solution)/shard_map/all_to_all | solution.py:12
  203.3 0.2 broadcast_in_dim.20
  203.5 32.2 %all_to_all.56 = bf16[8,32,8,512]{3,2,1,0:T(8,128)(2,1)S(1)} all-to-all(bf16[8,32,8,512]{3,2,1,0:T(8,128)(2,1)S(1)} %broadcast_in_dim.20), channel_id=1, replica_groups=mesh['gx'=8,'gy_0'=4,'gy_1'=2,'gz'=4] {'gy_1','gz'}, dimensions={0} | all-to-all | bytes 4194304 | tf_op jit(solution)/shard_map/all_to_all | solution.py:12
  235.8 0.0 copy-start.6
  235.8 0.0 copy-start.9
  235.8 0.3 copy.26
  236.0 1.4 copy-done.6
  237.4 0.1 copy-done.9
  237.6 2.9 add_convert_fusion
  240.4 59.6 %all-gather.2.cloned.1.call-done = bf16[2048,1024]{1,0:T(8,128)(2,1)} async-done(((bf16[8,1024]{1,0:T(8,128)(2,1)}), bf16[2048,1024]{1,0:T(8,128)(2,1)}) %all-gather.2.cloned.1.call-update) | async-done | bytes 4194320 | tf_op jit(solution)/shard_map/all_gather | solution.py:75
  300.1 4.5 %fusion.5 = (bf16[2048,512]{1,0:T(8,128)(2,1)}, bf16[2048,512]{1,0:T(8,128)(2,1)}) fusion(bf16[2048,1024]{1,0:T(8,128)(2,1)} %all-gather.2.cloned.1.call-done), kind=kLoop, calls=%fused_computation.22 | loop fusion | bytes 8388608 | tf_op jit(solution)/shard_map/split | solution.py:75
  (7 shorter events, 0.2 us)
Async XLA Ops:
  7.2 68.5 %copy-start = (bf16[588,2048]{1,0:T(8,128)(2,1)S(1)}, bf16[588,2048]{1,0:T(8,128)(2,1)}, u32[]{:S(2)}) copy-start(bf16[588,2048]{1,0:T(8,128)(2,1)} %param.7) | copy-start | bytes 7225348
  33.3 6.9 %copy-start.7 = (bf16[588,512]{1,0:T(8,128)(2,1)S(1)}, bf16[588,512]{1,0:T(8,128)(2,1)}, u32[]{:S(2)}) copy-start(bf16[588,512]{1,0:T(8,128)(2,1)} %param.8) | copy-start | bytes 1806340
  33.3 33.2 %all-to-all-start.1 = ((bf16[8,32,8,512]{3,2,1,0:T(8,128)(2,1)}), bf16[8,32,8,512]{3,2,1,0:T(8,128)(2,1)}, u32[]{:S(2)}, u32[]{:S(2)}) async-start(bf16[8,32,8,512]{3,2,1,0:T(8,128)(2,1)} %broadcast_in_dim.17), calls=%async_computation.1 | async-start | bytes 4194304 | tf_op jit(solution)/shard_map/all_to_all | solution.py:12
  66.5 30.8 %all-to-all-start.4 = ((bf16[8,32,8,512]{3,2,1,0:T(8,128)(2,1)}), bf16[8,32,8,512]{3,2,1,0:T(8,128)(2,1)}, u32[]{:S(2)}, u32[]{:S(2)}) async-start(bf16[8,32,8,512]{3,2,1,0:T(8,128)(2,1)} %bitcast.31), calls=%async_computation.4 | async-start | bytes 4194304 | tf_op jit(solution)/shard_map/all_to_all | solution.py:37
  71.0 2.3 copy-start.5
  74.8 0.8 copy-start.8
  97.4 30.9 %all-to-all-start.6 = ((bf16[8,32,8,512]{3,2,1,0:T(8,128)(2,1)}), bf16[8,32,8,512]{3,2,1,0:T(8,128)(2,1)}, u32[]{:S(2)}, u32[]{:S(2)}) async-start(bf16[8,32,8,512]{3,2,1,0:T(8,128)(2,1)} %copy.29), calls=%async_computation.6 | async-start | bytes 4194304 | tf_op jit(solution)/shard_map/all_to_all | solution.py:37
  104.6 43.7 %copy-start.2 = (f32[8,512]{1,0:T(8,128)S(1)}, f32[8,512]{1,0:T(8,128)}, u32[]{:S(2)}) copy-start(f32[8,512]{1,0:T(8,128)} %param.10) | copy-start | bytes 49156
  104.6 83.3 %copy-start.1 = (f32[8,512]{1,0:T(8,128)S(1)}, f32[8,512]{1,0:T(8,128)}, u32[]{:S(2)}) copy-start(f32[8,512]{1,0:T(8,128)} %param.11) | copy-start | bytes 49156
  104.6 83.3 %copy-start.3 = (f32[8,512]{1,0:T(8,128)S(1)}, f32[8,512]{1,0:T(8,128)}, u32[]{:S(2)}) copy-start(f32[8,512]{1,0:T(8,128)} %param.13) | copy-start | bytes 49156
  104.6 83.9 %copy-start.4 = (f32[8,512]{1,0:T(8,128)S(1)}, f32[8,512]{1,0:T(8,128)}, u32[]{:S(2)}) copy-start(f32[8,512]{1,0:T(8,128)} %param.12) | copy-start | bytes 49156
  128.2 15.6 %all-to-all-start.5 = ((bf16[32,8,512]{2,1,0:T(8,128)(2,1)}), bf16[32,8,512]{2,1,0:T(8,128)(2,1)S(1)}, u32[]{:S(2)}, u32[]{:S(2)}) async-start(bf16[32,8,512]{2,1,0:T(8,128)(2,1)} %reduce_sum.97), calls=%async_computation.5 | async-start | bytes 524288 | tf_op jit(solution)/shard_map/all_to_all | solution.py:45
  143.8 14.8 %all-to-all-start.7 = ((bf16[32,8,512]{2,1,0:T(8,128)(2,1)}), bf16[32,8,512]{2,1,0:T(8,128)(2,1)S(1)}, u32[]{:S(2)}, u32[]{:S(2)}) async-start(bf16[32,8,512]{2,1,0:T(8,128)(2,1)} %reduce_sum.101), calls=%async_computation.7 | async-start | bytes 524288 | tf_op jit(solution)/shard_map/all_to_all | solution.py:45
  148.2 151.9 %all-gather.2.cloned.1.call-start = ((), (), s32[]{:S(2)}) async-start(), calls=%async_computation.10 | async-start | bytes 4210688 | tf_op jit(solution)/shard_map/all_gather | solution.py:75
  235.8 1.7 copy-start.6
  235.8 1.8 copy-start.9
Sparse Core Ops, SparseCore 0:
  189.9 110.1 all-gather.1
where the time goes:
time: 312 us; the launch traced here: 311 us
  waiting for transfers between devices  134 us (43%)
  blocking collectives  91.3 us (29%)
  starting transfers between devices  24.2 us (8%)
  local copies, waits for them, and re-layouts  20.3 us (7%)
  between operations  17 us (5%)
  other arithmetic  13.3 us (4%)
  matrix products  11 us (4%)
    all_to_all x5, blocking collectives, from_everyone(): lax.all_to_all(jnp.broadcast_to(array[None], (peers, *array.shape)), axis...  91.3 us
    all_gather x1, waiting for transfers between devices, sent_together(): lax.all_gather(both, axis, axis=dim, tiled=True)  59.6 us
    all_to_all x2, waiting for transfers between devices, summed_on_arrival(): parts = lax.all_to_all(split_up(array, dim, peers), axis, 0, 0, tiled=True)  35.2 us
    all_to_all x1, waiting for transfers between devices, from_everyone(): lax.all_to_all(jnp.broadcast_to(array[None], (peers, *array.shape)), axis...  21.2 us
    all_to_all x2, waiting for transfers between devices, summed_rows(): lax.all_to_all(nearer.astype(jnp.bfloat16), far, split_axis=0, concat_axi...  18.2 us
    all_to_all x2, starting transfers between devices, summed_on_arrival(): parts = lax.all_to_all(split_up(array, dim, peers), axis, 0, 0, tiled=True)  9.1 us
    all_to_all x2, starting transfers between devices, summed_rows(): lax.all_to_all(nearer.astype(jnp.bfloat16), far, split_axis=0, concat_axi...  8.22 us
    all_to_all x1, starting transfers between devices, from_everyone(): lax.all_to_all(jnp.broadcast_to(array[None], (peers, *array.shape)), axis...  6.89 us
  transfers between devices with their start and end apart: 6, of which 6 were waited for; matrix products, arithmetic and copies ran while one was open for 9% of the time, Pallas kernels for 0%

commit v1 on v0

v1 whole, which is shorter than its diff:
```python
import jax
import jax.numpy as jnp
from jax import lax
from jax.experimental import pallas as pl
from jax.experimental.pallas import tpu as pltpu
from jax.sharding import PartitionSpec as P

MESH = pl.DeviceIdType.MESH
BF16 = jnp.bfloat16
F32 = jnp.float32
ROWS_SPLIT = ("gx", "gy", "gz")
NZ, NY, NX, NK = 8, 4, 4, 2
BLK = 8
SEMS = 320


class Net:
    def __init__(self, send, recv):
        self.send, self.recv, self.used = send, recv, 0

    def put(self, src, dst, peer):
        at = self.used
        self.used += 1
        copy = pltpu.make_async_remote_copy(
            src_ref=src,
            dst_ref=dst,
            send_sem=self.send.at[at],
            recv_sem=self.recv.at[at],
            device_id=peer,
            device_id_type=MESH,
        )
        copy.start()
        return copy


class Place:
    def __init__(self):
        self.z = lax.axis_index("gx")
        gy = lax.axis_index("gy")
        self.y = gy // 2
        self.k = gy % 2
        self.x = lax.axis_index("gz")
        self.gy = gy
        self.kx = self.k * NX + self.x
        self.d = 1 - 2 * self.k

    def zp(self, j):
        return {"gx": (self.z + j) % NZ}

    def yp(self, j):
        return {"gy": ((self.y + j + NY) % NY) * 2 + self.k}

    def xp(self, j):
        return {"gz": (self.x + j + NX) % NX}

    def other(self):
        return {"gy": self.gy + 1 - 2 * self.k}


class Gather:
    def __init__(self, net, me, w):
        self.net, self.me, self.w = net, me, w
        cols = w.shape[-1]
        half = cols // 2
        self.parts = (pl.ds(0, half), pl.ds(half, half))
        self.cores = []
        self.sent = []

    def put(self, ref, peer):
        copy = self.net.put(ref, ref, peer)
        self.sent.append(copy)
        return copy

    def along_z(self):
        me = self.me
        ref = self.w.at[me.z, me.y, me.kx]
        self.zs = [self.put(ref, me.zp(j)) for j in (4, 3, 5, 2, 6, 1, 7)]

    def middle(self):
        me = self.me
        for copy in self.zs:
            copy.wait_recv()
        self.mids = []
        for part, peer in zip(self.parts, (me.yp, me.xp)):
            ref = self.w.at[:, me.y, me.kx, :, part]
            self.mids.append([self.put(ref, peer(j)) for j in (2, 1, 3)])

    def slab(self, part, off):
        me = self.me
        if part == 0:
            x = (me.x + off + NX) % NX
            return self.w.at[:, :, me.k * NX + x, :, self.parts[0]]
        y = (me.y + off + NY) % NY
        return self.w.at[:, y, pl.ds(me.k * NX, NX), :, self.parts[1]]

    def peer(self, part, off):
        return self.me.xp(off) if part == 0 else self.me.yp(off)

    def core(self, part, off):
        self.cores.append(self.put(self.slab(part, off), self.me.other()))

    def large(self):
        d = self.me.d
        self.near = []
        for part in range(2):
            for copy in self.mids[part]:
                copy.wait_recv()
            ref = self.slab(part, 0)
            self.near.append((self.put(ref, self.peer(part, d)), self.put(ref, self.peer(part, -d))))
            self.core(part, 0)

    def forward(self):
        d = self.me.d
        self.far = []
        for part in range(2):
            self.near[part][0].wait_recv()
            self.far.append(self.put(self.slab(part, -d), self.peer(part, d)))
            self.core(part, -d)

    def finish(self):
        d = self.me.d
        for part in range(2):
            self.near[part][1].wait_recv()
            self.core(part, d)
        for part in range(2):
            self.far[part].wait_recv()
            self.core(part, 2)

    def arrived(self):
        for copy in self.cores:
            copy.wait_recv()

    def drain(self):
        for copy in self.sent:
            copy.wait_send()


def add_blocks(count, out, *terms):
    def step(i, carry):
        total = terms[0](i).astype(F32)
        for term in terms[1:]:
            total = total + term(i).astype(F32)
        out(i, total)
        return carry

    lax.fori_loop(0, count, step, 0)


class Scatter:
    def __init__(self, net, me, refs):
        self.net, self.me = net, me
        (self.p, self.c, self.s, self.f, self.t, self.r, self.a, self.m, self.b, self.q) = refs
        self.sent = []

    def put(self, src, dst, peer):
        copy = self.net.put(src, dst, peer)
        self.sent.append(copy)
        return copy

    def tile(self, t, value):
        half = value.shape[1] // 2
        for y in range(NY):
            for k in range(NK):
                for x in range(NX):
                    at = ((y * NK + k) * NX + x) * BLK
                    rows = value[at : at + BLK]
                    self.p[0, k, x, y * NZ + t] = rows[:, :half].astype(BF16)
                    self.p[1, k, y, x * NZ + t] = rows[:, half:].astype(BF16)

    def cores(self):
        me = self.me
        self.cs = [
            self.put(self.p.at[part, 1 - me.k], self.c.at[part], me.other()) for part in range(2)
        ]

    def peer(self, part, off):
        return self.me.xp(off) if part == 0 else self.me.yp(off)

    def index(self, part, off):
        return (self.me.x + off + NX) % NX if part == 0 else (self.me.y + off + NY) % NY

    def large(self):
        me = self.me
        d = me.d
        self.near = []
        for part in range(2):
            self.cs[part].wait_recv()
            first = self.put(self.joined(part, 2), self.f.at[part], self.peer(part, d))
            second = self.put(self.joined(part, -d), self.r.at[part, 0], self.peer(part, -d))
            self.near.append((first, second))
        for part in range(2):
            self.joined(part, d)
            self.joined(part, 0)

    def joined(self, part, off):
        me = self.me
        at = self.index(part, off)

        def out(i, total):
            self.s[part, at, pl.ds(i * 8, 8)] = total.astype(BF16)

        add_blocks(
            4,
            out,
            lambda i: self.p[part, me.k, at, pl.ds(i * 8, 8)],
            lambda i: self.c[part, at, pl.ds(i * 8, 8)],
        )
        return self.s.at[part, at]

    def forward(self):
        d = self.me.d
        self.far = []
        for part in range(2):
            self.near[part][0].wait_recv()
            at = self.index(part, d)

            def out(i, total, part=part):
                self.t[part, pl.ds(i * 8, 8)] = total.astype(BF16)

            add_blocks(
                4,
                out,
                lambda i, part=part, at=at: self.s[part, at, pl.ds(i * 8, 8)],
                lambda i, part=part: self.f[part, pl.ds(i * 8, 8)],
            )
            self.far.append(self.put(self.t.at[part], self.r.at[part, 1], self.peer(part, d)))

    def middle(self):
        me = self.me
        self.mids = []
        for part in range(2):
            self.near[part][1].wait_recv()
            self.far[part].wait_recv()
            at = self.index(part, 0)

            def out(i, total, part=part):
                self.a[part, pl.ds(i * 8, 8)] = total.astype(BF16)

            add_blocks(
                4,
                out,
                lambda i, part=part, at=at: self.s[part, at, pl.ds(i * 8, 8)],
                lambda i, part=part: self.r[part, 0, pl.ds(i * 8, 8)],
                lambda i, part=part: self.r[part, 1, pl.ds(i * 8, 8)],
            )
            copies = []
            for j in (2, 1, 3):
                to = self.index(1 - part, j)
                copies.append(
                    self.put(
                        self.a.at[part, pl.ds(to * 8, 8)],
                        self.m.at[part, j - 1],
                        self.peer(1 - part, j),
                    )
                )
            self.mids.append(copies)

    def along_z(self):
        me = self.me
        for part in range(2):
            for copy in self.mids[part]:
                copy.wait_recv()
            at = self.index(1 - part, 0)
            total = self.a[part, pl.ds(at * 8, 8)].astype(F32)
            for j in range(3):
                total = total + self.m[part, j].astype(F32)
            half = total.shape[-1]
            self.b[:, :, pl.ds(part * half, half)] = total.astype(BF16)
        self.zs = []
        for j in (4, 3, 5, 2, 6, 1, 7):
            self.zs.append(self.put(self.b.at[(me.z + j) % NZ], self.q.at[j - 1], me.zp(j)))

    def result(self):
        for copy in self.zs:
            copy.wait_recv()
        total = self.b[self.me.z].astype(F32)
        for j in range(7):
            total = total + self.q[j].astype(F32)
        return total

    def drain(self):
        for copy in self.sent:
            copy.wait_send()


class Norms:
    def __init__(self, net, me, refs):
        self.net, self.me, self.refs = net, me, refs
        self.sent = []

    def start(self, axis, tile):
        me = self.me
        ref = self.refs[axis]
        own = (me.z, me.y, me.x, me.k)[axis]
        ref[own] = tile
        peers = (
            [me.zp(j) for j in (4, 3, 5, 2, 6, 1, 7)],
            [me.yp(j) for j in (2, 1, 3)],
            [me.xp(j) for j in (2, 1, 3)],
            [me.other()],
        )[axis]
        self.flying = [self.net.put(ref.at[own], ref.at[own], peer) for peer in peers]
        self.sent += self.flying

    def finish(self, axis):
        ref = self.refs[axis]
        for copy in self.flying:
            copy.wait_recv()
        total = ref[0]
        for i in range(1, ref.shape[0]):
            total = total + ref[i]
        return total

    def drain(self):
        for copy in self.sent:
            copy.wait_send()


def fold(sq):
    lanes = sq[:, 0:128]
    for i in range(1, sq.shape[1] // 128):
        lanes = lanes + sq[:, 128 * i : 128 * (i + 1)]
    return jnp.sum(lanes, axis=0, keepdims=True)


def stat_tile(w, g):
    row = lax.broadcasted_iota(jnp.int32, (8, 128), 0)
    wrow = jnp.broadcast_to(fold(w * w), (8, 128))
    grow = jnp.broadcast_to(fold(g * g), (8, 128))
    return jnp.where(row == 0, wrow, jnp.where(row == 1, grow, 0.0))


def updated(master, grads, velocity, tile):
    wsquare = jnp.sum(tile[0:1, :], axis=1, keepdims=True)
    gsquare = jnp.sum(tile[1:2, :], axis=1, keepdims=True)
    wnorm = jnp.sqrt(wsquare)
    gnorm = jnp.sqrt(gsquare)
    trust = wnorm / (gnorm + 5e-05 * wnorm)
    new_velocity = 0.9 * velocity + trust * (grads + 5e-05 * master)
    new_master = master - 0.1 * new_velocity
    return new_master, new_velocity


def kernel(
    acts_h, hid_h, go_h, mr_h, me_h, vr_h, ve_h,
    gi_h, nmr_h, nme_h, nvr_h, nve_h, wr_h, we_h,
    acts, hid, go, small, smallout, gi, gh, acc,
    we, wr, ne, nr, flat, ge_refs, gr_refs, nz_e, nz_r,
    send, recv, load, out_sem,
):
    me = Place()
    net = Net(send, recv)
    channels = go.shape[1]
    middle = hid.shape[1]
    inv_c = 1.0 / float(channels) ** 0.5
    inv_m = 1.0 / float(middle) ** 0.5

    loads = [
        pltpu.make_async_copy(src, dst, load.at[i])
        for i, (src, dst) in enumerate(
            (
                (me_h, small.at[0]),
                (mr_h, small.at[1]),
                (go_h, go),
                (hid_h, hid),
                (ve_h, small.at[2]),
                (vr_h, small.at[3]),
                (acts_h, acts),
            )
        )
    ]
    for copy in loads:
        copy.start()

    barrier = pltpu.get_barrier_semaphore()
    peers = [me.zp(j) for j in range(1, NZ)] + [me.yp(j) for j in range(1, NY)]
    peers += [me.xp(j) for j in range(1, NX)] + [me.other()]
    for peer in peers:
        pl.semaphore_signal(barrier, inc=1, device_id=peer, device_id_type=MESH)

    loads[0].wait()
    loads[1].wait()
    we[me.z, me.y, me.kx] = small[0].astype(BF16)
    wr[me.z, me.y, me.kx] = small[1].astype(BF16)
    pl.semaphore_wait(barrier, len(peers))

    gather_e = Gather(net, me, we)
    gather_r = Gather(net, me, wr)
    gather_ne = Gather(net, me, ne)
    gather_nr = Gather(net, me, nr)
    scatter_e = Scatter(net, me, ge_refs)
    scatter_r = Scatter(net, me, gr_refs)
    norms_e = Norms(net, me, nz_e)
    norms_r = Norms(net, me, nz_r)
    tiles = channels // 256

    gather_e.along_z()
    loads[2].wait()
    loads[3].wait()

    def ge_tile(t, carry):
        cols = go[:, pl.ds(pl.multiple_of(t * 256, 256), 256)]
        value = lax.dot_general(
            cols, hid[...], (((0,), (0,)), ((), ())), preferred_element_type=F32
        )
        scatter_e.tile(t, value * inv_m)
        return carry

    lax.fori_loop(0, tiles, ge_tile, 0)
    scatter_e.cores()
    gather_e.middle()
    gather_r.along_z()
    gather_e.large()
    gather_r.middle()
    gather_e.forward()
    scatter_e.large()
    gather_e.finish()
    gather_e.arrived()

    def natural(w, t):
        block = w[t].reshape(NY * NK * NX, BLK, middle)
        return block.astype(F32).reshape(256, middle).astype(BF16)

    def flatten(t, carry):
        flat[pl.ds(pl.multiple_of(t * 256, 256), 256), :] = natural(we, t)
        return carry

    lax.fori_loop(0, tiles, flatten, 0)
    acc[...] = jnp.dot(go[...], flat[...], preferred_element_type=F32)
    gh[...] = jnp.where(hid[...].astype(F32) > 0, acc[...] * inv_m, 0.0).astype(BF16)
    loads[6].wait()

    def gr_tile(t, carry):
        cols = acts[:, pl.ds(pl.multiple_of(t * 256, 256), 256)]
        value = lax.dot_general(
            cols, gh[...], (((0,), (0,)), ((), ())), preferred_element_type=F32
        )
        scatter_r.tile(t, value * inv_c)
        return carry

    lax.fori_loop(0, tiles, gr_tile, 0)
    scatter_r.cores()
    scatter_e.forward()
    scatter_r.large()
    scatter_e.middle()
    scatter_r.forward()
    scatter_e.along_z()
    scatter_r.middle()
    gather_r.large()

    g_e = scatter_e.result()
    loads[4].wait()
    loads[5].wait()
    smallout[0] = g_e
    norms_e.start(0, stat_tile(small[0], g_e))
    scatter_r.along_z()
    tile_e = norms_e.finish(0)
    norms_e.start(1, tile_e)
    gather_r.forward()
    tile_e = norms_e.finish(1)
    norms_e.start(2, tile_e)
    g_r = scatter_r.result()
    norms_r.start(0, stat_tile(small[1], g_r))
    tile_e = norms_e.finish(2)
    norms_e.start(3, tile_e)
    tile_e = norms_e.finish(3)
    new_me, new_ve = updated(small[0], smallout[0], small[2], tile_e)
    ne[me.z, me.y, me.kx] = new_me.astype(BF16)
    gather_ne.along_z()
    smallout[0] = new_me
    smallout[1] = new_ve
    tile_r = norms_r.finish(0)
    norms_r.start(1, tile_r)
    gather_r.finish()
    tile_r = norms_r.finish(1)
    norms_r.start(2, tile_r)
    tile_r = norms_r.finish(2)
    norms_r.start(3, tile_r)
    tile_r = norms_r.finish(3)
    new_mr, new_vr = updated(small[1], g_r, small[3], tile_r)
    nr[me.z, me.y, me.kx] = new_mr.astype(BF16)
    gather_nr.along_z()
    smallout[2] = new_mr
    smallout[3] = new_vr
    gather_ne.middle()
    gather_ne.large()
    gather_nr.middle()
    gather_r.arrived()

    def gi_tile(t, carry):
        cols = pl.ds(pl.multiple_of(t * 256, 256), 256)
        back = lax.dot_general(
            gh[...], natural(wr, t), (((1,), (1,)), ((), ())), preferred_element_type=F32
        )
        gi[:, cols] = (go[:, cols].astype(F32) + back * inv_c).astype(BF16)
        return carry

    lax.fori_loop(0, tiles, gi_tile, 0)
    outs = [
        pltpu.make_async_copy(src, dst, out_sem.at[i])
        for i, (src, dst) in enumerate(
            (
                (gi, gi_h),
                (smallout.at[0], nme_h),
                (smallout.at[1], nve_h),
                (smallout.at[2], nmr_h),
                (smallout.at[3], nvr_h),
                (ne, we_h),
                (nr, wr_h),
            )
        )
    ]
    for copy in outs[:5]:
        copy.start()
    gather_ne.forward()
    gather_nr.large()
    gather_ne.finish()
    gather_nr.forward()
    gather_ne.arrived()
    outs[5].start()
    gather_nr.finish()
    gather_nr.arrived()
    outs[6].start()
    for unit in (
        gather_e, gather_r, gather_ne, gather_nr, scatter_e, scatter_r, norms_e, norms_r
    ):
        unit.drain()
    for copy in outs:
        copy.wait()
    assert net.used <= SEMS


def shards(acts, hid, go, mr, me_, vr, ve):
    rows, channels = acts.shape
    middle = hid.shape[1]
    half = middle // 2
    own = mr.shape
    whole = (NZ, NY, NK * NX, BLK, middle)
    scatter = (
        pltpu.VMEM((2, NK, 4, 32, BLK, half), BF16),
        pltpu.VMEM((2, 4, 32, BLK, half), BF16),
        pltpu.VMEM((2, 4, 32, BLK, half), BF16),
        pltpu.VMEM((2, 32, BLK, half), BF16),
        pltpu.VMEM((2, 32, BLK, half), BF16),
        pltpu.VMEM((2, 2, 32, BLK, half), BF16),
        pltpu.VMEM((2, 32, BLK, half), BF16),
        pltpu.VMEM((2, 3, NZ, BLK, half), BF16),
        pltpu.VMEM((NZ, BLK, middle), BF16),
        pltpu.VMEM((NZ - 1, BLK, middle), BF16),
    )
    norms = tuple(pltpu.VMEM((n, 8, 128), F32) for n in (NZ, NY, NX, NK))
    anyspace = pl.BlockSpec(memory_space=pl.ANY)
    out = pl.pallas_call(
        kernel,
        out_shape=(
            jax.ShapeDtypeStruct((rows, channels), BF16),
            jax.ShapeDtypeStruct(own, F32),
            jax.ShapeDtypeStruct(own, F32),
            jax.ShapeDtypeStruct(own, F32),
            jax.ShapeDtypeStruct(own, F32),
            jax.ShapeDtypeStruct(whole, BF16),
            jax.ShapeDtypeStruct(whole, BF16),
        ),
        in_specs=[anyspace] * 7,
        out_specs=(anyspace,) * 7,
        scratch_shapes=[
            pltpu.VMEM((rows, channels), BF16),
            pltpu.VMEM((rows, middle), BF16),
            pltpu.VMEM((rows, channels), BF16),
            pltpu.VMEM((4, *own), F32),
            pltpu.VMEM((4, *own), F32),
            pltpu.VMEM((rows, channels), BF16),
            pltpu.VMEM((rows, middle), BF16),
            pltpu.VMEM((rows, middle), F32),
            pltpu.VMEM(whole, BF16),
            pltpu.VMEM(whole, BF16),
            pltpu.VMEM(whole, BF16),
            pltpu.VMEM(whole, BF16),
            pltpu.VMEM((channels, middle), BF16),
            scatter,
            scatter,
            norms,
            norms,
            pltpu.SemaphoreType.DMA((SEMS,)),
            pltpu.SemaphoreType.DMA((SEMS,)),
            pltpu.SemaphoreType.DMA((7,)),
            pltpu.SemaphoreType.DMA((7,)),
        ],
        compiler_params=pltpu.CompilerParams(
            collective_id=0, has_side_effects=True, vmem_limit_bytes=60 * 1024 * 1024
        ),
    )(acts, hid, go, mr, me_, vr, ve)
    flat = (channels, middle)
    return (*out[:5], out[5].reshape(flat), out[6].reshape(flat))


def solution(mesh):
    split = P(ROWS_SPLIT, None)
    return jax.shard_map(
        shards,
        mesh=mesh,
        in_specs=(split,) * 7,
        out_specs=(split,) * 5 + (P(), P()),
        check_vma=False,
    )
```

time: 312 us -> 109 us (0.35)
  waiting for transfers between devices: 134 us -> 0 us
  Pallas kernels: 0 us -> 99 us
  blocking collectives: 91.3 us -> 0 us
  starting transfers between devices: 24.2 us -> 0 us
  between operations: 17 us -> 0.69 us
  other arithmetic: 13.3 us -> 0 us
  local copies, waits for them, and re-layouts: 20.3 us -> 8.64 us
  matrix products: 11 us -> 0 us
    pallas_call x0 -> x1, Pallas kernels: none -> 99 us  [shards(): pl.pallas_call(kernel, out_shape=(jax.ShapeDtypeStruct((rows, channels),...]
    all_to_all x5 -> x0, blocking collectives: 91.3 us -> none  [from_everyone(): lax.all_to_all(jnp.broadcast_to(array[None], (peers, *array.shape)), axis...]
    all_to_all x5 -> x0, waiting for transfers between devices: 74.6 us -> none  [the longest x2 35.2 us: summed_on_arrival(): parts = lax.all_to_all(split_up(array, dim, peers), axis, 0, 0, tiled=True)]
    all_gather x1 -> x0, waiting for transfers between devices: 59.6 us -> none  [sent_together(): lax.all_gather(both, axis, axis=dim, tiled=True)]
    all_to_all x5 -> x0, starting transfers between devices: 24.2 us -> none  [the longest x2 9.1 us: summed_on_arrival(): parts = lax.all_to_all(split_up(array, dim, peers), axis, 0, 0, tiled=True)]
    dot_general x4 -> x0, matrix products: 11 us -> none  [the longest x1 3.52 us: shards(): lax.dot_general(columns, saved_hidden, (((0,), (0,)), ((), ())), preferre...]
    reduce_sum x10 -> x0, other arithmetic: 8.8 us -> none  [the longest x2 5.32 us: summed_on_arrival(): return jnp.sum(parts.astype(jnp.float32), axis=0)]
    unnamed x20 -> x19, local copies, waits for them, and re-layouts: 2.68 us -> 8.64 us
  transfers between devices with their start and end apart: 6 -> 0, of which waited for: 6 -> 0; matrix products, arithmetic and copies ran while one was open for 9% -> 0% of each run, Pallas kernels for 0% -> 0%
where the time goes in v1:
time: 109 us; the launch traced here: 108 us
  Pallas kernels  99 us (91%)
  local copies, waits for them, and re-layouts  8.64 us (8%)
    pallas_call x1, Pallas kernels, shards(): pl.pallas_call(kernel, out_shape=(jax.ShapeDtypeStruct((rows, channels),...  99 us
    unnamed x19, local copies, waits for them, and re-layouts  8.64 us

profile of v1, /device:TPU:1, one launch (start us, length us, event | category | flops | bytes accessed | tf_op | source)
XLA Modules:
  0.0 108.3 jit_solution(6659340258940287123)
XLA Ops:
  0.6 99.0 %shard_map.126 = (bf16[588,2048]{1,0:T(8,128)(2,1)}, f32[8,512]{1,0:T(8,128)}, f32[8,512]{1,0:T(8,128)}, f32[8,512]{1,0:T(8,128)}, f32[8,512]{1,0:T(8,128)}, /*i...) custom-call(bf16[588,2048]{1,0:T(8,128)(2,1)} %acts_h.1, bf16[588,512]{1,0:T(8,128)(2,1)} %hid_h.1, ...), custom_call_target="tpu_custom_call" | custom-call | tf_op jit(solution)/shard_map/pallas_call | solution.py:553
  99.7 0.0 copy-start.5
  99.7 0.0 copy-start.4
  99.7 0.0 copy-start.3
  99.7 0.0 copy-start.2
  99.7 0.0 copy-start.1
  99.7 3.6 %copy.21 = bf16[588,2048]{1,0:T(8,128)(2,1)} copy(bf16[588,2048]{1,0:T(8,128)(2,1)} %get-tuple-element.28) | data formatting | bytes 4816896
  103.3 0.0 copy-done.5
  103.3 0.0 copy-start
  103.3 0.6 copy.22
  103.9 0.0 copy-done.4
  103.9 0.6 copy.23
  104.5 0.0 copy-done.3
  104.5 0.6 copy.24
  105.1 0.0 copy-done.2
  105.1 0.6 copy.25
  105.7 0.0 copy-done.1
  105.7 1.3 %copy.26 = bf16[2048,512]{1,0:T(8,128)(2,1)} copy(bf16[2048,512]{1,0:T(8,128)(2,1)S(1)} %bitcast.3) | data formatting | bytes 4194304
  107.0 0.0 copy-done
  107.0 1.3 %copy.27 = bf16[2048,512]{1,0:T(8,128)(2,1)} copy(bf16[2048,512]{1,0:T(8,128)(2,1)S(1)} %bitcast.2) | data formatting | bytes 4194304
Async XLA Ops:
  99.7 3.6 %copy-start.5 = (f32[8,512]{1,0:T(8,128)S(1)}, f32[8,512]{1,0:T(8,128)}, u32[]{:S(2)}) copy-start(f32[8,512]{1,0:T(8,128)} %get-tuple-element.29) | copy-start | bytes 49156
  99.7 4.2 %copy-start.4 = (f32[8,512]{1,0:T(8,128)S(1)}, f32[8,512]{1,0:T(8,128)}, u32[]{:S(2)}) copy-start(f32[8,512]{1,0:T(8,128)} %get-tuple-element.30) | copy-start | bytes 49156
  99.7 4.8 %copy-start.3 = (f32[8,512]{1,0:T(8,128)S(1)}, f32[8,512]{1,0:T(8,128)}, u32[]{:S(2)}) copy-start(f32[8,512]{1,0:T(8,128)} %get-tuple-element.31) | copy-start | bytes 49156
  99.7 5.4 %copy-start.2 = (f32[8,512]{1,0:T(8,128)S(1)}, f32[8,512]{1,0:T(8,128)}, u32[]{:S(2)}) copy-start(f32[8,512]{1,0:T(8,128)} %get-tuple-element.32) | copy-start | bytes 49156
  99.7 6.0 %copy-start.1 = (bf16[8,4,8,8,512]{4,3,2,1,0:T(8,128)(2,1)S(1)}, bf16[8,4,8,8,512]{4,3,2,1,0:T(8,128)(2,1)}, u32[]{:S(2)}) copy-start(bf16[8,4,8,8,512]{4,3,2,1,0:T(8,128)(2,1)} %get-tuple-element.19) | copy-start | bytes 6291460
  103.3 3.8 %copy-start = (bf16[8,4,8,8,512]{4,3,2,1,0:T(8,128)(2,1)S(1)}, bf16[8,4,8,8,512]{4,3,2,1,0:T(8,128)(2,1)}, u32[]{:S(2)}) copy-start(bf16[8,4,8,8,512]{4,3,2,1,0:T(8,128)(2,1)} %get-tuple-element.20) | copy-start | bytes 6291460

commit v2 on v1

v2 whole, which is shorter than its diff:
```python
import jax
import jax.numpy as jnp
from jax import lax
from jax.experimental import pallas as pl
from jax.experimental.pallas import tpu as pltpu
from jax.sharding import PartitionSpec as P

MESH = pl.DeviceIdType.MESH
BF16 = jnp.bfloat16
F32 = jnp.float32
ROWS_SPLIT = ("gx", "gy", "gz")
NZ, NY, NX, NK = 8, 4, 4, 2
BLK = 8
FAR_FIRST = (4, 3, 5, 2, 6, 1, 7)
SEMS = 400
CHUNKS = 2


class Net:
    def __init__(self, send, recv):
        self.send, self.recv, self.used = send, recv, 0

    def put(self, src, dst, peer):
        at = self.used
        self.used += 1
        copy = pltpu.make_async_remote_copy(
            src_ref=src,
            dst_ref=dst,
            send_sem=self.send.at[at],
            recv_sem=self.recv.at[at],
            device_id=peer,
            device_id_type=MESH,
        )
        copy.start()
        return copy


class Place:
    def __init__(self):
        self.z = lax.axis_index("gx")
        gy = lax.axis_index("gy")
        self.y = gy // 2
        self.k = gy % 2
        self.x = lax.axis_index("gz")
        self.gy = gy
        self.kx = self.k * NX + self.x
        self.d = 1 - 2 * self.k

    def zp(self, j):
        return {"gx": (self.z + j) % NZ}

    def yp(self, j):
        return {"gy": ((self.y + j + NY) % NY) * 2 + self.k}

    def xp(self, j):
        return {"gz": (self.x + j + NX) % NX}

    def other(self):
        return {"gy": self.gy + 1 - 2 * self.k}


class Gather:
    def __init__(self, net, me, w):
        self.net, self.me, self.w = net, me, w
        half = w.shape[-1] // 2
        self.parts = (pl.ds(0, half), pl.ds(half, half))
        self.cores = []
        self.sent = []

    def put(self, ref, peer):
        copy = self.net.put(ref, ref, peer)
        self.sent.append(copy)
        return copy

    def along_z(self):
        me = self.me
        ref = self.w.at[me.z, me.y, me.kx]
        self.zs = [self.put(ref, me.zp(j)) for j in FAR_FIRST]

    def middle(self):
        me = self.me
        for copy in self.zs:
            copy.wait_recv()
        self.mids = []
        for part, peer in zip(self.parts, (me.yp, me.xp)):
            ref = self.w.at[:, me.y, me.kx, :, part]
            self.mids.append([self.put(ref, peer(j)) for j in (2, 1, 3)])

    def slab(self, part, off, chunk=None):
        me = self.me
        zs = slice(None)
        if chunk is not None:
            zs = pl.ds(chunk * (NZ // CHUNKS), NZ // CHUNKS)
        if part == 0:
            x = (me.x + off + NX) % NX
            return self.w.at[zs, :, me.k * NX + x, :, self.parts[0]]
        y = (me.y + off + NY) % NY
        return self.w.at[zs, y, pl.ds(me.k * NX, NX), :, self.parts[1]]

    def peer(self, part, off):
        return self.me.xp(off) if part == 0 else self.me.yp(off)

    def core(self, part, off, chunk=None):
        self.cores.append(self.put(self.slab(part, off, chunk), self.me.other()))

    def middle_arrived(self, part):
        for copy in self.mids[part]:
            copy.wait_recv()

    def large(self):
        d = self.me.d
        self.near = []
        for part in range(2):
            self.middle_arrived(part)
            ahead = [
                self.put(self.slab(part, 0, c), self.peer(part, d)) for c in range(CHUNKS)
            ]
            self.near.append((ahead, self.put(self.slab(part, 0), self.peer(part, -d))))
        for part in range(2):
            self.core(part, 0)

    def forward(self):
        d = self.me.d
        self.far = ([], [])
        for c in range(CHUNKS):
            for part in range(2):
                self.near[part][0][c].wait_recv()
                self.far[part].append(self.put(self.slab(part, -d, c), self.peer(part, d)))
        for part in range(2):
            self.core(part, -d)

    def finish(self):
        d = self.me.d
        for part in range(2):
            self.near[part][1].wait_recv()
            self.core(part, d)
        for c in range(CHUNKS):
            for part in range(2):
                self.far[part][c].wait_recv()
                self.core(part, 2, c)

    def arrived(self):
        for copy in self.cores:
            copy.wait_recv()

    def drain(self):
        for copy in self.sent:
            copy.wait_send()


class Strips:
    def __init__(self, net, me, zb, m):
        self.net, self.me, self.zb, self.m = net, me, zb, m
        self.sent = []

    def along_z(self, block):
        me = self.me
        self.zb[me.z] = block
        ref = self.zb.at[me.z]
        self.zs = [self.net.put(ref, ref, me.zp(j)) for j in FAR_FIRST]
        self.sent += self.zs

    def middle(self):
        me = self.me
        half = self.m.shape[-1]
        for copy in self.zs:
            copy.wait_recv()
        self.mids = []
        for part, peer, own in ((0, me.yp, me.y), (1, me.xp, me.x)):
            src = self.zb.at[:, :, pl.ds(part * half, half)]
            self.mids += [self.net.put(src, self.m.at[part, own], peer(j)) for j in (2, 1, 3)]
        self.sent += self.mids
        for part, own in ((0, me.y), (1, me.x)):
            self.m[part, own] = self.zb[:, :, pl.ds(part * half, half)]

    def arrived(self):
        for copy in self.mids:
            copy.wait_recv()

    def drain(self):
        for copy in self.sent:
            copy.wait_send()


def add_blocks(first, last, out, *terms):
    def step(i, carry):
        total = terms[0](i).astype(F32)
        for term in terms[1:]:
            total = total + term(i).astype(F32)
        out(i, total)
        return carry

    lax.fori_loop(first, last, step, 0)


class Scatter:
    def __init__(self, net, me, refs):
        self.net, self.me = net, me
        (self.p, self.c, self.s, self.f, self.t, self.r, self.a, self.m, self.b, self.q) = refs
        self.sent = []
        self.cs = ([], [])

    def put(self, src, dst, peer):
        copy = self.net.put(src, dst, peer)
        self.sent.append(copy)
        return copy

    def tile(self, t, value):
        half = value.shape[1] // 2
        for y in range(NY):
            for k in range(NK):
                for x in range(NX):
                    at = ((y * NK + k) * NX + x) * BLK
                    rows = value[at : at + BLK]
                    self.p[0, k, x, y, t] = rows[:, :half].astype(BF16)
                    self.p[1, k, y, x, t] = rows[:, half:].astype(BF16)

    def cores(self, first, count):
        me = self.me
        for part in range(2):
            zs = pl.ds(first, count)
            self.cs[part].append(
                self.put(
                    self.p.at[part, 1 - me.k, :, :, zs], self.c.at[part, :, :, zs], me.other()
                )
            )

    def peer(self, part, off):
        return self.me.xp(off) if part == 0 else self.me.yp(off)

    def index(self, part, off):
        return (self.me.x + off + NX) % NX if part == 0 else (self.me.y + off + NY) % NY

    def joined(self, part, off, first=0, count=4):
        me = self.me
        at = self.index(part, off)

        def out(i, total):
            self.s[part, at, i] = total.astype(BF16)

        add_blocks(
            first,
            first + count,
            out,
            lambda i: self.p[part, me.k, at, i],
            lambda i: self.c[part, at, i],
        )
        return self.s.at[part, at, pl.ds(first, count)]

    def large(self):
        d = self.me.d
        per = 4 // CHUNKS
        self.near = ([], [])
        for part in range(2):
            for copy in self.cs[part]:
                copy.wait_recv()
        for c in range(CHUNKS):
            for part in range(2):
                src = self.joined(part, 2, c * per, per)
                dst = self.f.at[part, pl.ds(c * per, per)]
                self.near[part].append(self.put(src, dst, self.peer(part, d)))
        self.side = [
            self.put(self.joined(part, -d), self.r.at[part, 0], self.peer(part, -d))
            for part in range(2)
        ]
        for part in range(2):
            self.joined(part, d)
            self.joined(part, 0)

    def forward(self):
        d = self.me.d
        per = 4 // CHUNKS
        self.far = ([], [])
        for c in range(CHUNKS):
            for part in range(2):
                self.near[part][c].wait_recv()
                at = self.index(part, d)

                def out(i, total, part=part):
                    self.t[part, i] = total.astype(BF16)

                add_blocks(
                    c * per,
                    (c + 1) * per,
                    out,
                    lambda i, part=part, at=at: self.s[part, at, i],
                    lambda i, part=part: self.f[part, i],
                )
                piece = pl.ds(c * per, per)
                self.far[part].append(
                    self.put(
                        self.t.at[part, piece], self.r.at[part, 1, piece], self.peer(part, d)
                    )
                )

    def middle(self):
        self.mids = []
        for part in range(2):
            self.side[part].wait_recv()
            for copy in self.far[part]:
                copy.wait_recv()
            at = self.index(part, 0)

            def out(i, total, part=part):
                self.a[part, i] = total.astype(BF16)

            add_blocks(
                0,
                4,
                out,
                lambda i, part=part, at=at: self.s[part, at, i],
                lambda i, part=part: self.r[part, 0, i],
                lambda i, part=part: self.r[part, 1, i],
            )
            copies = []
            for j in (2, 1, 3):
                to = self.index(1 - part, j)
                copies.append(
                    self.put(self.a.at[part, to], self.m.at[part, j - 1], self.peer(1 - part, j))
                )
            self.mids.append(copies)

    def along_z(self):
        me = self.me
        for part in range(2):
            for copy in self.mids[part]:
                copy.wait_recv()
            at = self.index(1 - part, 0)
            total = self.a[part, at].astype(F32)
            for j in range(3):
                total = total + self.m[part, j].astype(F32)
            half = total.shape[-1]
            self.b[:, :, pl.ds(part * half, half)] = total.astype(BF16)
        self.zs = []
        for j in FAR_FIRST:
            self.zs.append(self.put(self.b.at[(me.z + j) % NZ], self.q.at[j - 1], me.zp(j)))

    def result(self):
        for copy in self.zs:
            copy.wait_recv()
        total = self.b[self.me.z].astype(F32)
        for j in range(7):
            total = total + self.q[j].astype(F32)
        return total

    def drain(self):
        for copy in self.sent:
            copy.wait_send()


class Norms:
    def __init__(self, net, me, refs):
        self.net, self.me, self.refs = net, me, refs
        self.sent = []

    def start(self, axis, tile):
        me = self.me
        ref = self.refs[axis]
        own = (me.z, me.y, me.x, me.k)[axis]
        ref[own] = tile
        peers = (
            [me.zp(j) for j in FAR_FIRST],
            [me.yp(j) for j in (2, 1, 3)],
            [me.xp(j) for j in (2, 1, 3)],
            [me.other()],
        )[axis]
        self.flying = [self.net.put(ref.at[own], ref.at[own], peer) for peer in peers]
        self.sent += self.flying

    def finish(self, axis):
        ref = self.refs[axis]
        for copy in self.flying:
            copy.wait_recv()
        total = ref[0]
        for i in range(1, ref.shape[0]):
            total = total + ref[i]
        return total

    def drain(self):
        for copy in self.sent:
            copy.wait_send()


def fold(sq):
    lanes = sq[:, 0:128]
    for i in range(1, sq.shape[1] // 128):
        lanes = lanes + sq[:, 128 * i : 128 * (i + 1)]
    return jnp.sum(lanes, axis=0, keepdims=True)


def stat_tile(w, g):
    row = lax.broadcasted_iota(jnp.int32, (8, 128), 0)
    wrow = jnp.broadcast_to(fold(w * w), (8, 128))
    grow = jnp.broadcast_to(fold(g * g), (8, 128))
    return jnp.where(row == 0, wrow, jnp.where(row == 1, grow, 0.0))


def trust_of(tile):
    wsquare = jnp.sum(tile[0:1, :], axis=1, keepdims=True)
    gsquare = jnp.sum(tile[1:2, :], axis=1, keepdims=True)
    wnorm = jnp.sqrt(wsquare)
    gnorm = jnp.sqrt(gsquare)
    return wnorm / (gnorm + 5e-05 * wnorm)


def updated(master, grads, velocity, trust):
    new_velocity = 0.9 * velocity + trust * (grads + 5e-05 * master)
    new_master = master - 0.1 * new_velocity
    return new_master, new_velocity


def kernel(
    acts_h, hid_h, go_h, mr_h, me_h, vr_h, ve_h,
    gi, smallout, ne, nr,
    acts, hid, go, small, gh, acc,
    we, wr, flat, g_kept, az, am, gz, gm, ge_refs, gr_refs, nz_e, nz_r,
    send, recv, load,
):
    scope = jax.named_scope
    me = Place()
    net = Net(send, recv)
    channels = go.shape[1]
    middle = hid.shape[1]
    half = middle // 2
    inv_c = 1.0 / float(channels) ** 0.5
    inv_m = 1.0 / float(middle) ** 0.5

    loads = [
        pltpu.make_async_copy(src, dst, load.at[i])
        for i, (src, dst) in enumerate(
            (
                (me_h, small.at[0]),
                (mr_h, small.at[1]),
                (vr_h, small.at[3]),
                (ve_h, small.at[2]),
                (go_h, go),
                (hid_h, hid),
                (acts_h, acts),
            )
        )
    ]
    for copy in loads:
        copy.start()

    barrier = pltpu.get_barrier_semaphore()
    peers = [me.zp(j) for j in FAR_FIRST] + [me.yp(j) for j in (2, 1, 3)]
    peers += [me.xp(j) for j in (2, 1, 3)] + [me.other()]
    for peer in peers:
        pl.semaphore_signal(barrier, inc=1, device_id=peer, device_id_type=MESH)

    for copy in loads[:4]:
        copy.wait()
    we[me.z, me.y, me.kx] = small[0].astype(BF16)
    wr[me.z, me.y, me.kx] = small[1].astype(BF16)
    with scope("barrier"):
        pl.semaphore_wait(barrier, len(peers))

    gather_e = Gather(net, me, we)
    gather_r = Gather(net, me, wr)
    gather_ne = Gather(net, me, ne)
    gather_nr = Gather(net, me, nr)
    scatter_e = Scatter(net, me, ge_refs)
    scatter_r = Scatter(net, me, gr_refs)
    norms_e = Norms(net, me, nz_e)
    norms_r = Norms(net, me, nz_r)
    strips_a = Strips(net, me, az, am)
    strips_g = Strips(net, me, gz, gm)
    tiles = channels // 256

    def tile_cols(t):
        return pl.ds(pl.multiple_of(t * 256, 256), 256)

    def natural(w, t):
        block = w[t].reshape(NY * NK * NX, BLK, middle)
        return block.astype(F32).reshape(256, middle).astype(BF16)

    def ge_tile(t, carry):
        value = lax.dot_general(
            go[:, tile_cols(t)], hid[...], (((0,), (0,)), ((), ())), preferred_element_type=F32
        )
        scatter_e.tile(t, value * inv_m)
        return carry

    def gr_tile(t, carry):
        value = lax.dot_general(
            acts[:, tile_cols(t)], gh[...], (((0,), (0,)), ((), ())), preferred_element_type=F32
        )
        scatter_r.tile(t, value * inv_c)
        return carry

    def flatten(t, carry):
        flat[tile_cols(t), :] = natural(we, t)
        return carry

    def gi_tile(t, carry):
        cols = tile_cols(t)
        back = lax.dot_general(
            gh[...], natural(wr, t), (((1,), (1,)), ((), ())), preferred_element_type=F32
        )
        gi[:, cols] = (go[:, cols].astype(F32) + back * inv_c).astype(BF16)
        return carry

    def e_result():
        g = scatter_e.result()
        g_kept[0] = g
        norms_e.start(0, stat_tile(small[0], g))

    def r_result():
        g = scatter_r.result()
        g_kept[1] = g
        norms_r.start(0, stat_tile(small[1], g))
        strips_g.along_z((g + 5e-05 * small[1]).astype(BF16))

    def norm_step(norms, axis):
        norms.start(axis + 1, norms.finish(axis))

    def e_update():
        trust = trust_of(norms_e.finish(3))
        new_master, new_velocity = updated(small[0], g_kept[0], small[2], trust)
        ne[me.z, me.y, me.kx] = new_master.astype(BF16)
        gather_ne.along_z()
        smallout[0] = new_master
        smallout[1] = new_velocity

    def r_update():
        trust = trust_of(norms_r.finish(3))
        strips_g.arrived()
        step = jnp.broadcast_to(0.1 * trust, (BLK, half))

        def fill(i, carry):
            for z in range(NZ):
                for part in range(2):
                    block = am[part, i, z] - step * gm[part, i, z].astype(F32)
                    if part == 0:
                        nr[z, i, me.kx, :, pl.ds(0, half)] = block.astype(BF16)
                    else:
                        nr[z, me.y, me.k * NX + i, :, pl.ds(half, half)] = block.astype(BF16)
            return carry

        lax.fori_loop(0, 4, fill, 0)
        gather_nr.mids = ([], [])
        gather_nr.large()
        new_master, new_velocity = updated(small[1], g_kept[1], small[3], trust)
        smallout[2] = new_master
        smallout[3] = new_velocity

    def ge_part(first, count):
        lax.fori_loop(first, first + count, ge_tile, 0)
        scatter_e.cores(first, count)

    def gr_part(first, count):
        lax.fori_loop(first, first + count, gr_tile, 0)
        scatter_r.cores(first, count)

    def hidden():
        lax.fori_loop(0, tiles, flatten, 0)
        acc[...] = jnp.dot(go[...], flat[...], preferred_element_type=F32)
        gh[...] = jnp.where(hid[...].astype(F32) > 0, acc[...] * inv_m, 0.0).astype(BF16)

    program = [
        ("E z", gather_e.along_z),
        ("R z", gather_r.along_z),
        ("A z", lambda: strips_a.along_z(small[1] - 0.09 * small[3])),
        ("load go", loads[4].wait),
        ("load hid", loads[5].wait),
        ("GE tiles 0", lambda: ge_part(0, 4)),
        ("GE tiles 1", lambda: ge_part(4, 4)),
        ("E mid", gather_e.middle),
        ("GE large", scatter_e.large),
        ("E large", gather_e.large),
        ("R mid", gather_r.middle),
        ("E forward", gather_e.forward),
        ("GE forward", scatter_e.forward),
        ("E finish", gather_e.finish),
        ("A mid", strips_a.middle),
        ("E arrived", gather_e.arrived),
        ("hidden", hidden),
        ("GE mid", scatter_e.middle),
        ("load acts", loads[6].wait),
        ("GR tiles 0", lambda: gr_part(0, 4)),
        ("GR tiles 1", lambda: gr_part(4, 4)),
        ("GE z", scatter_e.along_z),
        ("GR large", scatter_r.large),
        ("GE result", e_result),
        ("GR forward", scatter_r.forward),
        ("norm e0", lambda: norm_step(norms_e, 0)),
        ("GR mid", scatter_r.middle),
        ("R large", gather_r.large),
        ("norm e1", lambda: norm_step(norms_e, 1)),
        ("GR z", scatter_r.along_z),
        ("norm e2", lambda: norm_step(norms_e, 2)),
        ("R forward", gather_r.forward),
        ("E update", e_update),
        ("GR result", r_result),
        ("R finish", gather_r.finish),
        ("NE mid", gather_ne.middle),
        ("A arrived", strips_a.arrived),
        ("norm r0", lambda: norm_step(norms_r, 0)),
        ("g mid", strips_g.middle),
        ("NE large", gather_ne.large),
        ("norm r1", lambda: norm_step(norms_r, 1)),
        ("NE forward", gather_ne.forward),
        ("norm r2", lambda: norm_step(norms_r, 2)),
        ("R update", r_update),
        ("R arrived", gather_r.arrived),
        ("gi", lambda: lax.fori_loop(0, tiles, gi_tile, 0)),
        ("NR forward", gather_nr.forward),
        ("NE finish", gather_ne.finish),
        ("NR finish", gather_nr.finish),
        ("NE arrived", gather_ne.arrived),
        ("NR arrived", gather_nr.arrived),
    ]
    for name, step in program:
        with scope(name.replace(" ", "_")):
            step()
    with scope("drain"):
        for unit in (
            gather_e, gather_r, gather_ne, gather_nr, scatter_e, scatter_r,
            norms_e, norms_r, strips_a, strips_g,
        ):
            unit.drain()
    assert net.used <= SEMS


def write_out(gi, small, ne, nr, gi_h, nmr_h, nme_h, nvr_h, nve_h, wr_h, we_h, sem):
    copies = [
        pltpu.make_async_copy(src, dst, sem.at[i])
        for i, (src, dst) in enumerate(
            (
                (gi, gi_h),
                (ne, we_h),
                (nr, wr_h),
                (small.at[0], nme_h),
                (small.at[1], nve_h),
                (small.at[2], nmr_h),
                (small.at[3], nvr_h),
            )
        )
    ]
    for copy in copies:
        copy.start()
    for copy in copies:
        copy.wait()


def shards(acts, hid, go, mr, me_, vr, ve):
    rows, channels = acts.shape
    middle = hid.shape[1]
    half = middle // 2
    own = mr.shape
    whole = (NZ, NY, NK * NX, BLK, middle)
    scatter = (
        pltpu.VMEM((2, NK, 4, 4, NZ, BLK, half), BF16),
        pltpu.VMEM((2, 4, 4, NZ, BLK, half), BF16),
        pltpu.VMEM((2, 4, 4, NZ, BLK, half), BF16),
        pltpu.VMEM((2, 4, NZ, BLK, half), BF16),
        pltpu.VMEM((2, 4, NZ, BLK, half), BF16),
        pltpu.VMEM((2, 2, 4, NZ, BLK, half), BF16),
        pltpu.VMEM((2, 4, NZ, BLK, half), BF16),
        pltpu.VMEM((2, 3, NZ, BLK, half), BF16),
        pltpu.VMEM((NZ, BLK, middle), BF16),
        pltpu.VMEM((NZ - 1, BLK, middle), BF16),
    )
    norms = tuple(pltpu.VMEM((n, 8, 128), F32) for n in (NZ, NY, NX, NK))
    in_hbm = pl.BlockSpec(memory_space=pltpu.HBM)
    vmem = pl.BlockSpec(memory_space=pltpu.VMEM)
    results = pl.pallas_call(
        kernel,
        out_shape=(
            pltpu.VMEM((rows, channels), BF16),
            pltpu.VMEM((4, *own), F32),
            pltpu.VMEM(whole, BF16),
            pltpu.VMEM(whole, BF16),
        ),
        in_specs=[in_hbm] * 7,
        out_specs=(vmem,) * 4,
        scratch_shapes=[
            pltpu.VMEM((rows, channels), BF16),
            pltpu.VMEM((rows, middle), BF16),
            pltpu.VMEM((rows, channels), BF16),
            pltpu.VMEM((4, *own), F32),
            pltpu.VMEM((rows, middle), BF16),
            pltpu.VMEM((rows, middle), F32),
            pltpu.VMEM(whole, BF16),
            pltpu.VMEM(whole, BF16),
            pltpu.VMEM((channels, middle), BF16),
            pltpu.VMEM((2, *own), F32),
            pltpu.VMEM((NZ, BLK, middle), F32),
            pltpu.VMEM((2, 4, NZ, BLK, half), F32),
            pltpu.VMEM((NZ, BLK, middle), BF16),
            pltpu.VMEM((2, 4, NZ, BLK, half), BF16),
            scatter,
            scatter,
            norms,
            norms,
            pltpu.SemaphoreType.DMA((SEMS,)),
            pltpu.SemaphoreType.DMA((SEMS,)),
            pltpu.SemaphoreType.DMA((7,)),
        ],
        compiler_params=pltpu.CompilerParams(
            collective_id=0, has_side_effects=True, vmem_limit_bytes=44 * 1024 * 1024
        ),
    )(acts, hid, go, mr, me_, vr, ve)
    out = pl.pallas_call(
        write_out,
        out_shape=(
            jax.ShapeDtypeStruct((rows, channels), BF16),
            jax.ShapeDtypeStruct(own, F32),
            jax.ShapeDtypeStruct(own, F32),
            jax.ShapeDtypeStruct(own, F32),
            jax.ShapeDtypeStruct(own, F32),
            jax.ShapeDtypeStruct(whole, BF16),
            jax.ShapeDtypeStruct(whole, BF16),
        ),
        in_specs=[vmem] * 4,
        out_specs=(in_hbm,) * 7,
        scratch_shapes=[pltpu.SemaphoreType.DMA((7,))],
        compiler_params=pltpu.CompilerParams(vmem_limit_bytes=4 * 1024 * 1024),
    )(*results)
    flat = (channels, middle)
    return (*out[:5], out[5].reshape(flat), out[6].reshape(flat))


def solution(mesh):
    split = P(ROWS_SPLIT, None)
    return jax.shard_map(
        shards,
        mesh=mesh,
        in_specs=(split,) * 7,
        out_specs=(split,) * 5 + (P(), P()),
        check_vma=False,
    )
```

time: 109 us -> 95.5 us (0.88)
  Pallas kernels: 99 us -> 88.8 us
  local copies, waits for them, and re-layouts: 8.64 us -> 5.61 us
    pallas_call x1 -> x2, Pallas kernels: 99 us -> 88.8 us  [the longest x1 85.9 us: shards(): pl.pallas_call(kernel, out_shape=(pltpu.VMEM((rows, channels), BF16), plt...]
    unnamed x19 -> x12, local copies, waits for them, and re-layouts: 8.64 us -> 5.61 us
where the time goes in v2:
time: 95.5 us; the launch traced here: 95 us
  Pallas kernels  88.8 us (93%)
  local copies, waits for them, and re-layouts  5.61 us (6%)
    pallas_call x1, Pallas kernels, shards(): pl.pallas_call(kernel, out_shape=(pltpu.VMEM((rows, channels), BF16), plt...  85.9 us
    unnamed x12, local copies, waits for them, and re-layouts  5.61 us
    pallas_call x1, Pallas kernels, shards(): pl.pallas_call(write_out, out_shape=(jax.ShapeDtypeStruct((rows, channels...  2.88 us

profile of v2, /device:TPU:1, one launch (start us, length us, event | category | flops | bytes accessed | tf_op | source)
XLA Modules:
  0.0 95.0 jit_solution(4946080169081811681)
XLA Ops:
  0.6 0.0 copy-start
  0.6 1.7 %copy-done = bf16[588,2048]{1,0:T(8,128)(2,1)S(1)} copy-done((bf16[588,2048]{1,0:T(8,128)(2,1)S(1)}, bf16[588,2048]{1,0:T(8,128)(2,1)}, u32[]{:S(2)}) %copy-start) | copy-done | bytes 2408472
  2.3 0.0 copy-start.1
  2.3 1.1 %copy-done.1 = bf16[588,512]{1,0:T(8,128)(2,1)S(1)} copy-done((bf16[588,512]{1,0:T(8,128)(2,1)S(1)}, bf16[588,512]{1,0:T(8,128)(2,1)}, u32[]{:S(2)}) %copy-start.1) | copy-done | bytes 602136
  3.4 0.0 copy-start.2
  3.4 0.7 copy-done.2
  4.1 0.0 copy-start.3
  4.1 0.7 copy-done.3
  4.8 0.0 copy-start.4
  4.8 0.7 copy-done.4
  5.5 0.0 copy-start.5
  5.5 0.7 copy-done.5
  6.3 85.9 %shard_map.126 = (bf16[588,2048]{1,0:T(8,128)(2,1)S(1)}, f32[4,8,512]{2,1,0:T(8,128)S(1)}, bf16[8,4,8,8,512]{4,3,2,1,0:T(8,128)(2,1)S(1)}, bf16[8,4,8,8,512]{4,3,2,1,0:T(8,128)(2,1)S(1)}) custom-call(bf16[588,2048]{1,0:T(8,128)(2,1)S(1)} %copy-done, bf16[588,512]{1,0:T(8,128)(2,1)S(1)} %copy-done.1, bf16[588,2048]{1,0:T(8,128)(2,1)} %go_h.1, ...), custom_call_target="tpu_custom_call" | custom-call | tf_op jit(solution)/shard_map/pallas_call | solution.py:667
  92.2 2.9 %shard_map.127 = (bf16[588,2048]{1,0:T(8,128)(2,1)}, f32[8,512]{1,0:T(8,128)}, f32[8,512]{1,0:T(8,128)}, f32[8,512]{1,0:T(8,128)}, f32[8,512]{1,0:T(8,128)}, /*i...) custom-call(bf16[588,2048]{1,0:T(8,128)(2,1)S(1)} %get-tuple-element.18.gi, ...), custom_call_target="tpu_custom_call" | custom-call | tf_op jit(solution)/shard_map/pallas_call | solution.py:704
Async XLA Ops:
  0.6 1.7 %copy-start = (bf16[588,2048]{1,0:T(8,128)(2,1)S(1)}, bf16[588,2048]{1,0:T(8,128)(2,1)}, u32[]{:S(2)}) copy-start(bf16[588,2048]{1,0:T(8,128)(2,1)} %acts_h.1) | copy-start | bytes 7225348
  2.3 1.1 %copy-start.1 = (bf16[588,512]{1,0:T(8,128)(2,1)S(1)}, bf16[588,512]{1,0:T(8,128)(2,1)}, u32[]{:S(2)}) copy-start(bf16[588,512]{1,0:T(8,128)(2,1)} %hid_h.1) | copy-start | bytes 1806340
  3.4 0.7 copy-start.2
  4.1 0.7 copy-start.3
  4.8 0.7 copy-start.4
  5.5 0.7 copy-start.5

commit v3 on v2

--- a/solution.py
+++ b/solution.py
@@ -12,27 +12,53 @@
 NZ, NY, NX, NK = 8, 4, 4, 2
 BLK = 8
 FAR_FIRST = (4, 3, 5, 2, 6, 1, 7)
-SEMS = 400
-CHUNKS = 2
+STRIPS = (2, 1, 3, 0)
+SENDS = 10
+RECVS = 137
+MID_ORDER = (1, 3, 2)
+
+
+class Group:
+    def __init__(self, net, sem):
+        self.net, self.sem, self.bytes = net, sem, 0
+
+    def wait(self):
+        self.net.wait(self.sem, self.bytes)
 
 
 class Net:
-    def __init__(self, send, recv):
-        self.send, self.recv, self.used = send, recv, 0
-
-    def put(self, src, dst, peer):
-        at = self.used
+    def __init__(self, send, recv, spare):
+        self.send, self.recv, self.spare = send, recv, spare
+        self.used = self.units = 0
+
+    def unit(self):
+        self.units += 1
+        return Group(self, self.send.at[self.units - 1])
+
+    def group(self):
         self.used += 1
-        copy = pltpu.make_async_remote_copy(
+        return Group(self, self.recv.at[self.used - 1])
+
+    def put(self, src, dst, peer, unit, group):
+        size = src.dtype.itemsize
+        for extent in src.shape:
+            size *= extent
+        unit.bytes += size
+        group.bytes += size
+        pltpu.make_async_remote_copy(
             src_ref=src,
             dst_ref=dst,
-            send_sem=self.send.at[at],
-            recv_sem=self.recv.at[at],
+            send_sem=unit.sem,
+            recv_sem=group.sem,
             device_id=peer,
             device_id_type=MESH,
-        )
-        copy.start()
-        return copy
+        ).start()
+
+    def wait(self, sem, size):
+        blocks, rest = divmod(size, 4096)
+        assert rest == 0
+        ref = self.spare.at[pl.ds(0, blocks)]
+        pltpu.make_async_copy(ref, ref, sem).wait()
 
 
 class Place:
@@ -64,146 +90,144 @@
         self.net, self.me, self.w = net, me, w
         half = w.shape[-1] // 2
         self.parts = (pl.ds(0, half), pl.ds(half, half))
-        self.cores = []
-        self.sent = []
-
-    def put(self, ref, peer):
-        copy = self.net.put(ref, ref, peer)
-        self.sent.append(copy)
-        return copy
+        self.unit = net.unit()
+        self.cores = net.group()
+        self.ahead = ({}, {})
+        self.side = [net.group() for part in range(2)]
+        self.far = [[net.group(), net.group()] for part in range(2)]
+
+    def put(self, ref, peer, group):
+        self.net.put(ref, ref, peer, self.unit, group)
 
     def along_z(self):
         me = self.me
         ref = self.w.at[me.z, me.y, me.kx]
-        self.zs = [self.put(ref, me.zp(j)) for j in FAR_FIRST]
-
-    def middle(self):
+        self.zs = self.net.group()
+        for j in FAR_FIRST:
+            self.put(ref, me.zp(j), self.zs)
+
+    def at(self, part, large, mid):
         me = self.me
-        for copy in self.zs:
-            copy.wait_recv()
-        self.mids = []
-        for part, peer in zip(self.parts, (me.yp, me.xp)):
-            ref = self.w.at[:, me.y, me.kx, :, part]
-            self.mids.append([self.put(ref, peer(j)) for j in (2, 1, 3)])
-
-    def slab(self, part, off, chunk=None):
+        x = (me.x + (large if part == 0 else mid) + NX) % NX
+        y = (me.y + (mid if part == 0 else large) + NY) % NY
+        return self.w.at[:, y, me.k * NX + x, :, self.parts[part]]
+
+    def slab(self, part, off):
         me = self.me
-        zs = slice(None)
-        if chunk is not None:
-            zs = pl.ds(chunk * (NZ // CHUNKS), NZ // CHUNKS)
         if part == 0:
             x = (me.x + off + NX) % NX
-            return self.w.at[zs, :, me.k * NX + x, :, self.parts[0]]
+            return self.w.at[:, :, me.k * NX + x, :, self.parts[0]]
         y = (me.y + off + NY) % NY
-        return self.w.at[zs, y, pl.ds(me.k * NX, NX), :, self.parts[1]]
+        return self.w.at[:, y, pl.ds(me.k * NX, NX), :, self.parts[1]]
 
     def peer(self, part, off):
         return self.me.xp(off) if part == 0 else self.me.yp(off)
 
-    def core(self, part, off, chunk=None):
-        self.cores.append(self.put(self.slab(part, off, chunk), self.me.other()))
-
-    def middle_arrived(self, part):
-        for copy in self.mids[part]:
-            copy.wait_recv()
-
-    def large(self):
+    def core(self, ref):
+        self.put(ref, self.me.other(), self.cores)
+
+    def near(self, part, mid):
         d = self.me.d
-        self.near = []
+        self.ahead[part][mid] = self.net.group()
+        self.put(self.at(part, 0, mid), self.peer(part, d), self.ahead[part][mid])
+        self.put(self.at(part, 0, mid), self.peer(part, -d), self.side[part])
+
+    def middle(self):
+        self.zs.wait()
+        self.mids = [{j: self.net.group() for j in MID_ORDER} for part in range(2)]
+        for j in MID_ORDER:
+            for part in range(2):
+                self.put(self.at(part, 0, 0), self.peer(1 - part, j), self.mids[part][j])
         for part in range(2):
-            self.middle_arrived(part)
-            ahead = [
-                self.put(self.slab(part, 0, c), self.peer(part, d)) for c in range(CHUNKS)
-            ]
-            self.near.append((ahead, self.put(self.slab(part, 0), self.peer(part, -d))))
+            self.near(part, 0)
+
+    def near_one(self):
+        for j in (1, 3):
+            for part in range(2):
+                self.mids[part][j].wait()
+                self.near(part, -j)
+
+    def near_two(self):
         for part in range(2):
-            self.core(part, 0)
-
-    def forward(self):
+            self.mids[part][2].wait()
+            self.near(part, -2)
+        for part in range(2):
+            self.core(self.slab(part, 0))
+
+    def near_all(self):
+        for mid in (0, -1, -3, -2):
+            for part in range(2):
+                self.near(part, mid)
+        for part in range(2):
+            self.core(self.slab(part, 0))
+
+    def forward(self, *mids):
         d = self.me.d
-        self.far = ([], [])
-        for c in range(CHUNKS):
-            for part in range(2):
-                self.near[part][0][c].wait_recv()
-                self.far[part].append(self.put(self.slab(part, -d, c), self.peer(part, d)))
-        for part in range(2):
-            self.core(part, -d)
+        for mid in mids:
+            for part in range(2):
+                self.ahead[part][mid].wait()
+                group = self.far[part][0 if mid in (0, -1) else 1]
+                self.put(self.at(part, -d, mid), self.peer(part, d), group)
+        if -2 in mids:
+            for part in range(2):
+                self.core(self.slab(part, -d))
 
     def finish(self):
         d = self.me.d
         for part in range(2):
-            self.near[part][1].wait_recv()
-            self.core(part, d)
-        for c in range(CHUNKS):
-            for part in range(2):
-                self.far[part][c].wait_recv()
-                self.core(part, 2, c)
+            self.side[part].wait()
+            self.core(self.slab(part, d))
+        for i, mids in enumerate(((0, -1), (-3, -2))):
+            for part in range(2):
+                self.far[part][i].wait()
+                for mid in mids:
+                    self.core(self.at(part, 2, mid))
 
     def arrived(self):
-        for copy in self.cores:
-            copy.wait_recv()
-
-    def drain(self):
-        for copy in self.sent:
-            copy.wait_send()
+        self.cores.wait()
 
 
 class Strips:
     def __init__(self, net, me, zb, m):
         self.net, self.me, self.zb, self.m = net, me, zb, m
-        self.sent = []
+        self.unit, self.zs, self.mids = net.unit(), net.group(), net.group()
 
     def along_z(self, block):
         me = self.me
         self.zb[me.z] = block
         ref = self.zb.at[me.z]
-        self.zs = [self.net.put(ref, ref, me.zp(j)) for j in FAR_FIRST]
-        self.sent += self.zs
+        for j in FAR_FIRST:
+            self.net.put(ref, ref, me.zp(j), self.unit, self.zs)
 
     def middle(self):
         me = self.me
         half = self.m.shape[-1]
-        for copy in self.zs:
-            copy.wait_recv()
-        self.mids = []
-        for part, peer, own in ((0, me.yp, me.y), (1, me.xp, me.x)):
-            src = self.zb.at[:, :, pl.ds(part * half, half)]
-            self.mids += [self.net.put(src, self.m.at[part, own], peer(j)) for j in (2, 1, 3)]
-        self.sent += self.mids
+        self.zs.wait()
+        for j in (2, 1, 3):
+            for part, peer, own in ((0, me.yp, me.y), (1, me.xp, me.x)):
+                src = self.zb.at[:, :, pl.ds(part * half, half)]
+                self.net.put(src, self.m.at[part, own], peer(j), self.unit, self.mids)
         for part, own in ((0, me.y), (1, me.x)):
             self.m[part, own] = self.zb[:, :, pl.ds(part * half, half)]
 
     def arrived(self):
-        for copy in self.mids:
-            copy.wait_recv()
-
-    def drain(self):
-        for copy in self.sent:
-            copy.wait_send()
-
-
-def add_blocks(first, last, out, *terms):
-    def step(i, carry):
-        total = terms[0](i).astype(F32)
-        for term in terms[1:]:
-            total = total + term(i).astype(F32)
-        out(i, total)
-        return carry
-
-    lax.fori_loop(first, last, step, 0)
+        self.mids.wait()
 
 
 class Scatter:
     def __init__(self, net, me, refs):
         self.net, self.me = net, me
         (self.p, self.c, self.s, self.f, self.t, self.r, self.a, self.m, self.b, self.q) = refs
-        self.sent = []
-        self.cs = ([], [])
-
-    def put(self, src, dst, peer):
-        copy = self.net.put(src, dst, peer)
-        self.sent.append(copy)
-        return copy
+        self.unit = net.unit()
+        self.cs = net.group()
+        self.near = [[net.group() for mid in range(4)] for part in range(2)]
+        self.far = [[net.group() for mid in range(4)] for part in range(2)]
+        self.side = [net.group() for part in range(2)]
+        self.mids = [net.group() for part in range(2)]
+        self.zs = net.group()
+
+    def put(self, src, dst, peer, group):
+        self.net.put(src, dst, peer, self.unit, group)
 
     def tile(self, t, value):
         half = value.shape[1] // 2
@@ -217,12 +241,13 @@
 
     def cores(self, first, count):
         me = self.me
+        zs = pl.ds(first, count)
         for part in range(2):
-            zs = pl.ds(first, count)
-            self.cs[part].append(
-                self.put(
-                    self.p.at[part, 1 - me.k, :, :, zs], self.c.at[part, :, :, zs], me.other()
-                )
+            self.put(
+                self.p.at[part, 1 - me.k, :, :, zs],
+                self.c.at[part, :, :, zs],
+                me.other(),
+                self.cs,
             )
 
     def peer(self, part, off):
@@ -231,127 +256,83 @@
     def index(self, part, off):
         return (self.me.x + off + NX) % NX if part == 0 else (self.me.y + off + NY) % NY
 
-    def joined(self, part, off, first=0, count=4):
-        me = self.me
-        at = self.index(part, off)
-
-        def out(i, total):
-            self.s[part, at, i] = total.astype(BF16)
-
-        add_blocks(
-            first,
-            first + count,
-            out,
-            lambda i: self.p[part, me.k, at, i],
-            lambda i: self.c[part, at, i],
-        )
-        return self.s.at[part, at, pl.ds(first, count)]
+    def joined(self, part, off, mid):
+        at, i = self.index(part, off), self.index(1 - part, mid)
+        total = self.p[part, self.me.k, at, i].astype(F32) + self.c[part, at, i].astype(F32)
+        self.s[part, at, i] = total.astype(BF16)
+        return self.s.at[part, at, i]
 
     def large(self):
         d = self.me.d
-        per = 4 // CHUNKS
-        self.near = ([], [])
-        for part in range(2):
-            for copy in self.cs[part]:
-                copy.wait_recv()
-        for c in range(CHUNKS):
-            for part in range(2):
-                src = self.joined(part, 2, c * per, per)
-                dst = self.f.at[part, pl.ds(c * per, per)]
-                self.near[part].append(self.put(src, dst, self.peer(part, d)))
-        self.side = [
-            self.put(self.joined(part, -d), self.r.at[part, 0], self.peer(part, -d))
-            for part in range(2)
-        ]
-        for part in range(2):
-            self.joined(part, d)
-            self.joined(part, 0)
+        self.cs.wait()
+        for mid in STRIPS:
+            for part in range(2):
+                dst = self.f.at[part, self.index(1 - part, mid)]
+                src = self.joined(part, 2, mid)
+                self.put(src, dst, self.peer(part, d), self.near[part][mid])
+        for mid in STRIPS:
+            for part in range(2):
+                dst = self.r.at[part, 0, self.index(1 - part, mid)]
+                src = self.joined(part, -d, mid)
+                self.put(src, dst, self.peer(part, -d), self.side[part])
+        for mid in STRIPS:
+            for part in range(2):
+                self.joined(part, d, mid)
+                self.joined(part, 0, mid)
 
     def forward(self):
         d = self.me.d
-        per = 4 // CHUNKS
-        self.far = ([], [])
-        for c in range(CHUNKS):
-            for part in range(2):
-                self.near[part][c].wait_recv()
-                at = self.index(part, d)
-
-                def out(i, total, part=part):
-                    self.t[part, i] = total.astype(BF16)
-
-                add_blocks(
-                    c * per,
-                    (c + 1) * per,
-                    out,
-                    lambda i, part=part, at=at: self.s[part, at, i],
-                    lambda i, part=part: self.f[part, i],
-                )
-                piece = pl.ds(c * per, per)
-                self.far[part].append(
-                    self.put(
-                        self.t.at[part, piece], self.r.at[part, 1, piece], self.peer(part, d)
-                    )
-                )
+        for mid in STRIPS:
+            for part in range(2):
+                self.near[part][mid].wait()
+                i = self.index(1 - part, mid)
+                total = self.s[part, self.index(part, d), i].astype(F32)
+                total = total + self.f[part, i].astype(F32)
+                self.t[part, i] = total.astype(BF16)
+                dst = self.r.at[part, 1, i]
+                self.put(self.t.at[part, i], dst, self.peer(part, d), self.far[part][mid])
 
     def middle(self):
-        self.mids = []
         for part in range(2):
-            self.side[part].wait_recv()
-            for copy in self.far[part]:
-                copy.wait_recv()
-            at = self.index(part, 0)
-
-            def out(i, total, part=part):
+            self.side[part].wait()
+        for mid in STRIPS:
+            for part in range(2):
+                self.far[part][mid].wait()
+                i = self.index(1 - part, mid)
+                total = self.s[part, self.index(part, 0), i].astype(F32)
+                total = total + self.r[part, 0, i].astype(F32)
+                total = total + self.r[part, 1, i].astype(F32)
                 self.a[part, i] = total.astype(BF16)
-
-            add_blocks(
-                0,
-                4,
-                out,
-                lambda i, part=part, at=at: self.s[part, at, i],
-                lambda i, part=part: self.r[part, 0, i],
-                lambda i, part=part: self.r[part, 1, i],
-            )
-            copies = []
-            for j in (2, 1, 3):
-                to = self.index(1 - part, j)
-                copies.append(
-                    self.put(self.a.at[part, to], self.m.at[part, j - 1], self.peer(1 - part, j))
-                )
-            self.mids.append(copies)
+                if mid:
+                    dst = self.m.at[part, mid - 1]
+                    self.put(self.a.at[part, i], dst, self.peer(1 - part, mid), self.mids[part])
 
     def along_z(self):
         me = self.me
         for part in range(2):
-            for copy in self.mids[part]:
-                copy.wait_recv()
+            self.mids[part].wait()
             at = self.index(1 - part, 0)
             total = self.a[part, at].astype(F32)
             for j in range(3):
                 total = total + self.m[part, j].astype(F32)
             half = total.shape[-1]
             self.b[:, :, pl.ds(part * half, half)] = total.astype(BF16)
-        self.zs = []
         for j in FAR_FIRST:
-            self.zs.append(self.put(self.b.at[(me.z + j) % NZ], self.q.at[j - 1], me.zp(j)))
+            self.put(self.b.at[(me.z + j) % NZ], self.q.at[j - 1], me.zp(j), self.zs)
 
     def result(self):
-        for copy in self.zs:
-            copy.wait_recv()
+        self.zs.wait()
         total = self.b[self.me.z].astype(F32)
         for j in range(7):
             total = total + self.q[j].astype(F32)
         return total
 
-    def drain(self):
-        for copy in self.sent:
-            copy.wait_send()
-
 
 class Norms:
     def __init__(self, net, me, refs):
         self.net, self.me, self.refs = net, me, refs
-        self.sent = []
+        self.unit = net.unit()
+        self.groups = [net.group() for axis in range(4)]
 
     def start(self, axis, tile):
         me = self.me
@@ -364,21 +345,16 @@
             [me.xp(j) for j in (2, 1, 3)],
             [me.other()],
         )[axis]
-        self.flying = [self.net.put(ref.at[own], ref.at[own], peer) for peer in peers]
-        self.sent += self.flying
+        for peer in peers:
+            self.net.put(ref.at[own], ref.at[own], peer, self.unit, self.groups[axis])
 
     def finish(self, axis):
         ref = self.refs[axis]
-        for copy in self.flying:
-            copy.wait_recv()
+        self.groups[axis].wait()
         total = ref[0]
         for i in range(1, ref.shape[0]):
             total = total + ref[i]
         return total
-
-    def drain(self):
-        for copy in self.sent:
-            copy.wait_send()
 
 
 def fold(sq):
@@ -414,11 +390,11 @@
     gi, smallout, ne, nr,
     acts, hid, go, small, gh, acc,
     we, wr, flat, g_kept, az, am, gz, gm, ge_refs, gr_refs, nz_e, nz_r,
-    send, recv, load,
+    send, recv, load, spare,
 ):
     scope = jax.named_scope
     me = Place()
-    net = Net(send, recv)
+    net = Net(send, recv, spare)
     channels = go.shape[1]
     middle = hid.shape[1]
     half = middle // 2
@@ -538,8 +514,7 @@
             return carry
 
         lax.fori_loop(0, 4, fill, 0)
-        gather_nr.mids = ([], [])
-        gather_nr.large()
+        gather_nr.near_all()
         new_master, new_velocity = updated(small[1], g_kept[1], small[3], trust)
         smallout[2] = new_master
         smallout[3] = new_velocity
@@ -567,48 +542,54 @@
         ("GE tiles 1", lambda: ge_part(4, 4)),
         ("E mid", gather_e.middle),
         ("GE large", scatter_e.large),
-        ("E large", gather_e.large),
+        ("E near 1", gather_e.near_one),
+        ("E fwd 0", lambda: gather_e.forward(0)),
+        ("E near 2", gather_e.near_two),
+        ("E fwd 1", lambda: gather_e.forward(-1, -3)),
+        ("E fwd 2", lambda: gather_e.forward(-2)),
+        ("GE forward", scatter_e.forward),
         ("R mid", gather_r.middle),
-        ("E forward", gather_e.forward),
-        ("GE forward", scatter_e.forward),
         ("E finish", gather_e.finish),
-        ("A mid", strips_a.middle),
+        ("R near 1", gather_r.near_one),
+        ("R near 2", gather_r.near_two),
         ("E arrived", gather_e.arrived),
+        ("GE mid", scatter_e.middle),
         ("hidden", hidden),
-        ("GE mid", scatter_e.middle),
         ("load acts", loads[6].wait),
         ("GR tiles 0", lambda: gr_part(0, 4)),
+        ("R fwd", lambda: gather_r.forward(0, -1, -3, -2)),
         ("GR tiles 1", lambda: gr_part(4, 4)),
         ("GE z", scatter_e.along_z),
+        ("A mid", strips_a.middle),
         ("GR large", scatter_r.large),
+        ("GR forward", scatter_r.forward),
         ("GE result", e_result),
-        ("GR forward", scatter_r.forward),
+        ("GR mid", scatter_r.middle),
         ("norm e0", lambda: norm_step(norms_e, 0)),
-        ("GR mid", scatter_r.middle),
-        ("R large", gather_r.large),
+        ("R finish", gather_r.finish),
+        ("GR z", scatter_r.along_z),
         ("norm e1", lambda: norm_step(norms_e, 1)),
-        ("GR z", scatter_r.along_z),
         ("norm e2", lambda: norm_step(norms_e, 2)),
-        ("R forward", gather_r.forward),
+        ("GR result", r_result),
         ("E update", e_update),
-        ("GR result", r_result),
-        ("R finish", gather_r.finish),
-        ("NE mid", gather_ne.middle),
         ("A arrived", strips_a.arrived),
         ("norm r0", lambda: norm_step(norms_r, 0)),
         ("g mid", strips_g.middle),
-        ("NE large", gather_ne.large),
         ("norm r1", lambda: norm_step(norms_r, 1)),
-        ("NE forward", gather_ne.forward),
+        ("NE mid", gather_ne.middle),
         ("norm r2", lambda: norm_step(norms_r, 2)),
+        ("NE near 1", gather_ne.near_one),
         ("R update", r_update),
+        ("NE fwd 0", lambda: gather_ne.forward(0)),
+        ("NE near 2", gather_ne.near_two),
         ("R arrived", gather_r.arrived),
         ("gi", lambda: lax.fori_loop(0, tiles, gi_tile, 0)),
-        ("NR forward", gather_nr.forward),
+        ("NR fwd", lambda: gather_nr.forward(0, -1, -3, -2)),
+        ("NE fwd 1", lambda: gather_ne.forward(-1, -3, -2)),
+        ("NR finish", gather_nr.finish),
         ("NE finish", gather_ne.finish),
-        ("NR finish", gather_nr.finish),
+        ("NR arrived", gather_nr.arrived),
         ("NE arrived", gather_ne.arrived),
-        ("NR arrived", gather_nr.arrived),
     ]
     for name, step in program:
         with scope(name.replace(" ", "_")):
@@ -618,8 +599,8 @@
             gather_e, gather_r, gather_ne, gather_nr, scatter_e, scatter_r,
             norms_e, norms_r, strips_a, strips_g,
         ):
-            unit.drain()
-    assert net.used <= SEMS
+            unit.unit.wait()
+    assert (net.units, net.used) == (SENDS, RECVS)
 
 
 def write_out(gi, small, ne, nr, gi_h, nmr_h, nme_h, nvr_h, nve_h, wr_h, we_h, sem):
@@ -664,6 +645,7 @@
     norms = tuple(pltpu.VMEM((n, 8, 128), F32) for n in (NZ, NY, NX, NK))
     in_hbm = pl.BlockSpec(memory_space=pltpu.HBM)
     vmem = pl.BlockSpec(memory_space=pltpu.VMEM)
+    args = [pltpu.with_memory_space_constraint(a, pltpu.HBM) for a in (acts, hid, go, mr, me_, vr, ve)]
     results = pl.pallas_call(
         kernel,
         out_shape=(
@@ -693,14 +675,15 @@
             scatter,
             norms,
             norms,
-            pltpu.SemaphoreType.DMA((SEMS,)),
-            pltpu.SemaphoreType.DMA((SEMS,)),
+            pltpu.SemaphoreType.DMA((SENDS,)),
+            pltpu.SemaphoreType.DMA((RECVS,)),
             pltpu.SemaphoreType.DMA((7,)),
+            pltpu.VMEM((512, BLK, half), BF16),
         ],
         compiler_params=pltpu.CompilerParams(
             collective_id=0, has_side_effects=True, vmem_limit_bytes=44 * 1024 * 1024
         ),
-    )(acts, hid, go, mr, me_, vr, ve)
+    )(*args)
     out = pl.pallas_call(
         write_out,
         out_shape=(

time: 95.5 us -> 85.1 us (0.89)
  local copies, waits for them, and re-layouts: 5.61 us -> 0 us
  Pallas kernels: 88.8 us -> 84.3 us
    unnamed x12 -> x0, local copies, waits for them, and re-layouts: 5.61 us -> none
    pallas_call x1, Pallas kernels: 85.9 us -> 81.5 us  [shards(): pl.pallas_call(kernel, out_shape=(pltpu.VMEM((rows, channels), BF16), plt...]
where the time goes in v3:
time: 85.1 us; the launch traced here: 85 us
  Pallas kernels  84.3 us (99%)
    pallas_call x1, Pallas kernels, shards(): pl.pallas_call(kernel, out_shape=(pltpu.VMEM((rows, channels), BF16), plt...  81.5 us
    pallas_call x1, Pallas kernels, shards(): pl.pallas_call(write_out, out_shape=(jax.ShapeDtypeStruct((rows, channels...  2.88 us

profile of v3, /device:TPU:1, one launch (start us, length us, event | category | flops | bytes accessed | tf_op | source)
XLA Modules:
  0.0 85.0 jit_solution(1719889440726633122)
XLA Ops:
  0.6 81.5 %shard_map.126 = (bf16[588,2048]{1,0:T(8,128)(2,1)S(1)}, f32[4,8,512]{2,1,0:T(8,128)S(1)}, bf16[8,4,8,8,512]{4,3,2,1,0:T(8,128)(2,1)S(1)}, bf16[8,4,8,8,512]{4,3,2,1,0:T(8,128)(2,1)S(1)}) custom-call(bf16[588,2048]{1,0:T(8,128)(2,1)} %acts_h.1, bf16[588,512]{1,0:T(8,128)(2,1)} %hid_h.1, bf16[588,2048]{1,0:T(8,128)(2,1)} %go_h.1, f32[8,512]{1,0:T(8,128)} %mr_h.1, ...), custom_call_target="tpu_custom_call" | custom-call | tf_op jit(solution)/shard_map/pallas_call | solution.py:649
  82.1 2.9 %shard_map.127 = (bf16[588,2048]{1,0:T(8,128)(2,1)}, f32[8,512]{1,0:T(8,128)}, f32[8,512]{1,0:T(8,128)}, f32[8,512]{1,0:T(8,128)}, f32[8,512]{1,0:T(8,128)}, /*i...) custom-call(bf16[588,2048]{1,0:T(8,128)(2,1)S(1)} %get-tuple-element.18.gi, ...), custom_call_target="tpu_custom_call" | custom-call | tf_op jit(solution)/shard_map/pallas_call | solution.py:687

commit v4 on v3

--- a/solution.py
+++ b/solution.py
@@ -13,8 +13,9 @@
 BLK = 8
 FAR_FIRST = (4, 3, 5, 2, 6, 1, 7)
 STRIPS = (2, 1, 3, 0)
+PLANE = [(jy, jx) for jy in (2, 1, 3, 0) for jx in (2, 1, 3, 0)][:-1]
 SENDS = 10
-RECVS = 137
+RECVS = 120
 MID_ORDER = (1, 3, 2)
 
 
@@ -73,7 +74,11 @@
         self.d = 1 - 2 * self.k
 
     def zp(self, j):
-        return {"gx": (self.z + j) % NZ}
+        return {"gx": (self.z + j + NZ) % NZ}
+
+    def plane(self, jy, jk, jx):
+        y = (self.y + jy) % NY
+        return {"gy": y * NK + (self.k + jk) % NK, "gz": (self.x + jx) % NX}
 
     def yp(self, j):
         return {"gy": ((self.y + j + NY) % NY) * 2 + self.k}
@@ -182,6 +187,57 @@
                 self.far[part][i].wait()
                 for mid in mids:
                     self.core(self.at(part, 2, mid))
+
+    def arrived(self):
+        self.cores.wait()
+
+
+class GatherRound:
+    def __init__(self, net, me, w):
+        self.net, self.me, self.w = net, me, w
+        self.unit = net.unit()
+        self.blocks, self.cores, self.last = net.group(), net.group(), net.group()
+        self.up = [net.group() for step in range(3)]
+        self.down = [net.group() for step in range(3)]
+
+    def put(self, ref, peer, group):
+        self.net.put(ref, ref, peer, self.unit, group)
+
+    def plane(self):
+        me = self.me
+        ref = self.w.at[me.z, me.y, me.kx]
+        for jy, jx in PLANE:
+            self.put(ref, me.plane(jy, 0, jx), self.blocks)
+
+    def slab(self, off):
+        me = self.me
+        return self.w.at[(me.z + off + NZ) % NZ, :, pl.ds(me.k * NX, NX)]
+
+    def core(self, off):
+        self.put(self.slab(off), self.me.other(), self.cores)
+
+    def near(self):
+        self.blocks.wait()
+        self.put(self.slab(0), self.me.zp(1), self.up[0])
+        self.put(self.slab(0), self.me.zp(-1), self.down[0])
+        self.core(0)
+
+    def step(self, i):
+        self.up[i - 1].wait()
+        if i < 3:
+            self.put(self.slab(-i), self.me.zp(1), self.up[i])
+        self.down[i - 1].wait()
+        if i < 3:
+            self.put(self.slab(i), self.me.zp(-1), self.down[i])
+        else:
+            d = self.me.d
+            self.put(self.slab(-3 * d), self.me.zp(d), self.last)
+        self.core(-i)
+        self.core(i)
+
+    def finish(self):
+        self.last.wait()
+        self.core(4)
 
     def arrived(self):
         self.cores.wait()
@@ -332,48 +388,55 @@
     def __init__(self, net, me, refs):
         self.net, self.me, self.refs = net, me, refs
         self.unit = net.unit()
-        self.groups = [net.group() for axis in range(4)]
-
-    def start(self, axis, tile):
+        self.groups = [net.group() for axis in range(2)]
+
+    def start(self, axis, row):
         me = self.me
         ref = self.refs[axis]
-        own = (me.z, me.y, me.x, me.k)[axis]
-        ref[own] = tile
-        peers = (
-            [me.zp(j) for j in FAR_FIRST],
-            [me.yp(j) for j in (2, 1, 3)],
-            [me.xp(j) for j in (2, 1, 3)],
-            [me.other()],
-        )[axis]
+        own = me.gy * NX + me.x if axis else me.z
+        ref[own] = row
+        peers = [me.zp(j) for j in FAR_FIRST]
+        if axis:
+            peers = [me.plane(jy, 1, jx) for jy, jx in PLANE]
+            peers += [me.plane(jy, 0, jx) for jy, jx in PLANE] + [me.other()]
         for peer in peers:
             self.net.put(ref.at[own], ref.at[own], peer, self.unit, self.groups[axis])
 
     def finish(self, axis):
         ref = self.refs[axis]
-        self.groups[axis].wait()
+        self.wait(self.groups[axis].sem, ref.shape[0] - 1)
         total = ref[0]
         for i in range(1, ref.shape[0]):
             total = total + ref[i]
         return total
 
+    def wait(self, sem, count):
+        ref = self.refs[2].at[pl.ds(0, count)]
+        pltpu.make_async_copy(ref, ref, sem).wait()
+
+    def sent(self):
+        self.wait(self.unit.sem, NZ + NY * NX * NK - 2)
+
 
 def fold(sq):
     lanes = sq[:, 0:128]
     for i in range(1, sq.shape[1] // 128):
         lanes = lanes + sq[:, 128 * i : 128 * (i + 1)]
-    return jnp.sum(lanes, axis=0, keepdims=True)
-
-
-def stat_tile(w, g):
-    row = lax.broadcasted_iota(jnp.int32, (8, 128), 0)
-    wrow = jnp.broadcast_to(fold(w * w), (8, 128))
-    grow = jnp.broadcast_to(fold(g * g), (8, 128))
-    return jnp.where(row == 0, wrow, jnp.where(row == 1, grow, 0.0))
-
-
-def trust_of(tile):
-    wsquare = jnp.sum(tile[0:1, :], axis=1, keepdims=True)
-    gsquare = jnp.sum(tile[1:2, :], axis=1, keepdims=True)
+    row = jnp.sum(lanes, axis=0, keepdims=True)
+    return row + pltpu.roll(row, 64, 1)
+
+
+def low_lanes():
+    return lax.broadcasted_iota(jnp.int32, (1, 128), 1) < 64
+
+
+def stat_row(w, g):
+    return jnp.where(low_lanes(), fold(w * w), fold(g * g))
+
+
+def trust_of(row):
+    wsquare = jnp.sum(jnp.where(low_lanes(), row, 0.0), axis=1, keepdims=True)
+    gsquare = jnp.sum(jnp.where(low_lanes(), 0.0, row), axis=1, keepdims=True)
     wnorm = jnp.sqrt(wsquare)
     gnorm = jnp.sqrt(gsquare)
     return wnorm / (gnorm + 5e-05 * wnorm)
@@ -419,8 +482,8 @@
         copy.start()
 
     barrier = pltpu.get_barrier_semaphore()
-    peers = [me.zp(j) for j in FAR_FIRST] + [me.yp(j) for j in (2, 1, 3)]
-    peers += [me.xp(j) for j in (2, 1, 3)] + [me.other()]
+    peers = [me.zp(j) for j in FAR_FIRST] + [me.other()]
+    peers += [me.plane(jy, jk, jx) for jk in range(NK) for jy, jx in PLANE]
     for peer in peers:
         pl.semaphore_signal(barrier, inc=1, device_id=peer, device_id_type=MESH)
 
@@ -432,7 +495,7 @@
         pl.semaphore_wait(barrier, len(peers))
 
     gather_e = Gather(net, me, we)
-    gather_r = Gather(net, me, wr)
+    gather_r = GatherRound(net, me, wr)
     gather_ne = Gather(net, me, ne)
     gather_nr = Gather(net, me, nr)
     scatter_e = Scatter(net, me, ge_refs)
@@ -479,19 +542,19 @@
     def e_result():
         g = scatter_e.result()
         g_kept[0] = g
-        norms_e.start(0, stat_tile(small[0], g))
+        norms_e.start(0, stat_row(small[0], g))
 
     def r_result():
         g = scatter_r.result()
         g_kept[1] = g
-        norms_r.start(0, stat_tile(small[1], g))
+        norms_r.start(0, stat_row(small[1], g))
         strips_g.along_z((g + 5e-05 * small[1]).astype(BF16))
 
     def norm_step(norms, axis):
         norms.start(axis + 1, norms.finish(axis))
 
     def e_update():
-        trust = trust_of(norms_e.finish(3))
+        trust = trust_of(norms_e.finish(1))
         new_master, new_velocity = updated(small[0], g_kept[0], small[2], trust)
         ne[me.z, me.y, me.kx] = new_master.astype(BF16)
         gather_ne.along_z()
@@ -499,7 +562,7 @@
         smallout[1] = new_velocity
 
     def r_update():
-        trust = trust_of(norms_r.finish(3))
+        trust = trust_of(norms_r.finish(1))
         strips_g.arrived()
         step = jnp.broadcast_to(0.1 * trust, (BLK, half))
 
@@ -534,56 +597,52 @@
 
     program = [
         ("E z", gather_e.along_z),
-        ("R z", gather_r.along_z),
-        ("A z", lambda: strips_a.along_z(small[1] - 0.09 * small[3])),
+        ("R plane", gather_r.plane),
         ("load go", loads[4].wait),
         ("load hid", loads[5].wait),
         ("GE tiles 0", lambda: ge_part(0, 4)),
         ("GE tiles 1", lambda: ge_part(4, 4)),
         ("E mid", gather_e.middle),
-        ("GE large", scatter_e.large),
+        ("A z", lambda: strips_a.along_z(small[1] - 0.09 * small[3])),
         ("E near 1", gather_e.near_one),
+        ("R near", gather_r.near),
         ("E fwd 0", lambda: gather_e.forward(0)),
         ("E near 2", gather_e.near_two),
         ("E fwd 1", lambda: gather_e.forward(-1, -3)),
         ("E fwd 2", lambda: gather_e.forward(-2)),
+        ("GE large", scatter_e.large),
+        ("E finish", gather_e.finish),
+        ("R step 1", lambda: gather_r.step(1)),
+        ("E arrived", gather_e.arrived),
+        ("hidden", hidden),
+        ("A mid", strips_a.middle),
         ("GE forward", scatter_e.forward),
-        ("R mid", gather_r.middle),
-        ("E finish", gather_e.finish),
-        ("R near 1", gather_r.near_one),
-        ("R near 2", gather_r.near_two),
-        ("E arrived", gather_e.arrived),
-        ("GE mid", scatter_e.middle),
-        ("hidden", hidden),
         ("load acts", loads[6].wait),
         ("GR tiles 0", lambda: gr_part(0, 4)),
-        ("R fwd", lambda: gather_r.forward(0, -1, -3, -2)),
+        ("R step 2", lambda: gather_r.step(2)),
         ("GR tiles 1", lambda: gr_part(4, 4)),
+        ("GE mid", scatter_e.middle),
+        ("GR large", scatter_r.large),
         ("GE z", scatter_e.along_z),
-        ("A mid", strips_a.middle),
-        ("GR large", scatter_r.large),
         ("GR forward", scatter_r.forward),
+        ("R step 3", lambda: gather_r.step(3)),
+        ("GR mid", scatter_r.middle),
         ("GE result", e_result),
-        ("GR mid", scatter_r.middle),
-        ("norm e0", lambda: norm_step(norms_e, 0)),
+        ("GR z", scatter_r.along_z),
         ("R finish", gather_r.finish),
-        ("GR z", scatter_r.along_z),
-        ("norm e1", lambda: norm_step(norms_e, 1)),
-        ("norm e2", lambda: norm_step(norms_e, 2)),
+        ("norm e", lambda: norm_step(norms_e, 0)),
+        ("R arrived", gather_r.arrived),
         ("GR result", r_result),
+        ("A arrived", strips_a.arrived),
+        ("gi", lambda: lax.fori_loop(0, tiles, gi_tile, 0)),
         ("E update", e_update),
-        ("A arrived", strips_a.arrived),
-        ("norm r0", lambda: norm_step(norms_r, 0)),
+        ("norm r", lambda: norm_step(norms_r, 0)),
         ("g mid", strips_g.middle),
-        ("norm r1", lambda: norm_step(norms_r, 1)),
         ("NE mid", gather_ne.middle),
-        ("norm r2", lambda: norm_step(norms_r, 2)),
+        ("R update", r_update),
         ("NE near 1", gather_ne.near_one),
-        ("R update", r_update),
         ("NE fwd 0", lambda: gather_ne.forward(0)),
         ("NE near 2", gather_ne.near_two),
-        ("R arrived", gather_r.arrived),
-        ("gi", lambda: lax.fori_loop(0, tiles, gi_tile, 0)),
         ("NR fwd", lambda: gather_nr.forward(0, -1, -3, -2)),
         ("NE fwd 1", lambda: gather_ne.forward(-1, -3, -2)),
         ("NR finish", gather_nr.finish),
@@ -597,9 +656,11 @@
     with scope("drain"):
         for unit in (
             gather_e, gather_r, gather_ne, gather_nr, scatter_e, scatter_r,
-            norms_e, norms_r, strips_a, strips_g,
+            strips_a, strips_g,
         ):
             unit.unit.wait()
+        norms_e.sent()
+        norms_r.sent()
     assert (net.units, net.used) == (SENDS, RECVS)
 
 
@@ -642,7 +703,7 @@
         pltpu.VMEM((NZ, BLK, middle), BF16),
         pltpu.VMEM((NZ - 1, BLK, middle), BF16),
     )
-    norms = tuple(pltpu.VMEM((n, 8, 128), F32) for n in (NZ, NY, NX, NK))
+    norms = tuple(pltpu.VMEM((n, 1, 128), F32) for n in (NZ, NY * NX * NK, 40))
     in_hbm = pl.BlockSpec(memory_space=pltpu.HBM)
     vmem = pl.BlockSpec(memory_space=pltpu.VMEM)
     args = [pltpu.with_memory_space_constraint(a, pltpu.HBM) for a in (acts, hid, go, mr, me_, vr, ve)]

time: 85.1 us -> 78.6 us (0.924)
  Pallas kernels: 84.3 us -> 77.8 us
    pallas_call x1, Pallas kernels: 81.5 us -> 75 us  [shards(): pl.pallas_call(kernel, out_shape=(pltpu.VMEM((rows, channels), BF16), plt...]
where the time goes in v4:
time: 78.6 us; the launch traced here: 78.5 us
  Pallas kernels  77.8 us (99%)
    pallas_call x1, Pallas kernels, shards(): pl.pallas_call(kernel, out_shape=(pltpu.VMEM((rows, channels), BF16), plt...  75 us
    pallas_call x1, Pallas kernels, shards(): pl.pallas_call(write_out, out_shape=(jax.ShapeDtypeStruct((rows, channels...  2.88 us

profile of v4, /device:TPU:1, one launch (start us, length us, event | category | flops | bytes accessed | tf_op | source)
XLA Modules:
  0.0 78.5 jit_solution(3117371516428211493)
XLA Ops:
  0.6 75.0 %shard_map.126 = (bf16[588,2048]{1,0:T(8,128)(2,1)S(1)}, f32[4,8,512]{2,1,0:T(8,128)S(1)}, bf16[8,4,8,8,512]{4,3,2,1,0:T(8,128)(2,1)S(1)}, bf16[8,4,8,8,512]{4,3,2,1,0:T(8,128)(2,1)S(1)}) custom-call(bf16[588,2048]{1,0:T(8,128)(2,1)} %acts_h.1, bf16[588,512]{1,0:T(8,128)(2,1)} %hid_h.1, bf16[588,2048]{1,0:T(8,128)(2,1)} %go_h.1, f32[8,512]{1,0:T(8,128)} %mr_h.1, ...), custom_call_target="tpu_custom_call" | custom-call | tf_op jit(solution)/shard_map/pallas_call | solution.py:710
  75.6 2.9 %shard_map.127 = (bf16[588,2048]{1,0:T(8,128)(2,1)}, f32[8,512]{1,0:T(8,128)}, f32[8,512]{1,0:T(8,128)}, f32[8,512]{1,0:T(8,128)}, f32[8,512]{1,0:T(8,128)}, /*i...) custom-call(bf16[588,2048]{1,0:T(8,128)(2,1)S(1)} %get-tuple-element.18.gi, ...), custom_call_target="tpu_custom_call" | custom-call | tf_op jit(solution)/shard_map/pallas_call | solution.py:748

commit v5 on v4

--- a/solution.py
+++ b/solution.py
@@ -14,8 +14,8 @@
 FAR_FIRST = (4, 3, 5, 2, 6, 1, 7)
 STRIPS = (2, 1, 3, 0)
 PLANE = [(jy, jx) for jy in (2, 1, 3, 0) for jx in (2, 1, 3, 0)][:-1]
-SENDS = 10
-RECVS = 120
+SENDS = 12
+RECVS = 117
 MID_ORDER = (1, 3, 2)
 
 
@@ -326,6 +326,9 @@
                 dst = self.f.at[part, self.index(1 - part, mid)]
                 src = self.joined(part, 2, mid)
                 self.put(src, dst, self.peer(part, d), self.near[part][mid])
+
+    def aside(self):
+        d = self.me.d
         for mid in STRIPS:
             for part in range(2):
                 dst = self.r.at[part, 0, self.index(1 - part, mid)]
@@ -452,7 +455,7 @@
     acts_h, hid_h, go_h, mr_h, me_h, vr_h, ve_h,
     gi, smallout, ne, nr,
     acts, hid, go, small, gh, acc,
-    we, wr, flat, g_kept, az, am, gz, gm, ge_refs, gr_refs, nz_e, nz_r,
+    we, wr, flat, g_kept, az, am, gz, gm, turned, ge_refs, gr_refs, nz_e, nz_r,
     send, recv, load, spare,
 ):
     scope = jax.named_scope
@@ -502,8 +505,10 @@
     scatter_r = Scatter(net, me, gr_refs)
     norms_e = Norms(net, me, nz_e)
     norms_r = Norms(net, me, nz_r)
-    strips_a = Strips(net, me, az, am)
-    strips_g = Strips(net, me, gz, gm)
+    strips_ae = Strips(net, me, az.at[0], am.at[0])
+    strips_ar = Strips(net, me, az.at[1], am.at[1])
+    strips_ge = Strips(net, me, gz.at[0], gm.at[0])
+    strips_gr = Strips(net, me, gz.at[1], gm.at[1])
     tiles = channels // 256
 
     def tile_cols(t):
@@ -521,9 +526,7 @@
         return carry
 
     def gr_tile(t, carry):
-        value = lax.dot_general(
-            acts[:, tile_cols(t)], gh[...], (((0,), (0,)), ((), ())), preferred_element_type=F32
-        )
+        value = jnp.dot(turned[tile_cols(t), :], gh[...], preferred_element_type=F32)
         scatter_r.tile(t, value * inv_c)
         return carry
 
@@ -539,55 +542,52 @@
         gi[:, cols] = (go[:, cols].astype(F32) + back * inv_c).astype(BF16)
         return carry
 
-    def e_result():
-        g = scatter_e.result()
-        g_kept[0] = g
-        norms_e.start(0, stat_row(small[0], g))
-
-    def r_result():
-        g = scatter_r.result()
-        g_kept[1] = g
-        norms_r.start(0, stat_row(small[1], g))
-        strips_g.along_z((g + 5e-05 * small[1]).astype(BF16))
-
-    def norm_step(norms, axis):
-        norms.start(axis + 1, norms.finish(axis))
-
-    def e_update():
-        trust = trust_of(norms_e.finish(1))
-        new_master, new_velocity = updated(small[0], g_kept[0], small[2], trust)
-        ne[me.z, me.y, me.kx] = new_master.astype(BF16)
-        gather_ne.along_z()
-        smallout[0] = new_master
-        smallout[1] = new_velocity
-
-    def r_update():
-        trust = trust_of(norms_r.finish(1))
-        strips_g.arrived()
+    def far_term(i):
+        return (small[i] - 0.09 * small[i + 2]).astype(BF16)
+
+    def result(i, scatter, norms, strips):
+        g = scatter.result()
+        g_kept[i] = g
+        norms.start(0, stat_row(small[i], g))
+        strips.along_z((g + 5e-05 * small[i]).astype(BF16))
+
+    def norm_step(norms):
+        norms.start(1, norms.finish(0))
+
+    def update(i, out, norms, strips, gather):
+        trust = trust_of(norms.finish(1))
+        strips.arrived()
         step = jnp.broadcast_to(0.1 * trust, (BLK, half))
 
-        def fill(i, carry):
+        def fill(at, carry):
             for z in range(NZ):
                 for part in range(2):
-                    block = am[part, i, z] - step * gm[part, i, z].astype(F32)
+                    block = am[i, part, at, z].astype(F32) - step * gm[i, part, at, z].astype(F32)
                     if part == 0:
-                        nr[z, i, me.kx, :, pl.ds(0, half)] = block.astype(BF16)
+                        out[z, at, me.kx, :, pl.ds(0, half)] = block.astype(BF16)
                     else:
-                        nr[z, me.y, me.k * NX + i, :, pl.ds(half, half)] = block.astype(BF16)
+                        out[z, me.y, me.k * NX + at, :, pl.ds(half, half)] = block.astype(BF16)
             return carry
 
         lax.fori_loop(0, 4, fill, 0)
-        gather_nr.near_all()
-        new_master, new_velocity = updated(small[1], g_kept[1], small[3], trust)
-        smallout[2] = new_master
-        smallout[3] = new_velocity
+        gather.near_all()
+        new_master, new_velocity = updated(small[i], g_kept[i], small[i + 2], trust)
+        smallout[2 * i] = new_master
+        smallout[2 * i + 1] = new_velocity
+
+    def turn(first, count):
+        def one(t, carry):
+            turned[tile_cols(t), :] = acts[:, tile_cols(t)].T
+            return carry
+
+        lax.fori_loop(first, first + count, one, 0)
 
     def ge_part(first, count):
         lax.fori_loop(first, first + count, ge_tile, 0)
         scatter_e.cores(first, count)
 
     def gr_part(first, count):
-        lax.fori_loop(first, first + count, gr_tile, 0)
+        lax.fori_loop(first, first + count, gr_tile, 0, unroll=True)
         scatter_r.cores(first, count)
 
     def hidden():
@@ -603,52 +603,55 @@
         ("GE tiles 0", lambda: ge_part(0, 4)),
         ("GE tiles 1", lambda: ge_part(4, 4)),
         ("E mid", gather_e.middle),
-        ("A z", lambda: strips_a.along_z(small[1] - 0.09 * small[3])),
+        ("A z", lambda: (strips_ae.along_z(far_term(0)), strips_ar.along_z(far_term(1)))),
+        ("load acts", loads[6].wait),
+        ("turn 0", lambda: turn(0, 3)),
         ("E near 1", gather_e.near_one),
         ("R near", gather_r.near),
         ("E fwd 0", lambda: gather_e.forward(0)),
         ("E near 2", gather_e.near_two),
+        ("turn 1", lambda: turn(3, 3)),
         ("E fwd 1", lambda: gather_e.forward(-1, -3)),
         ("E fwd 2", lambda: gather_e.forward(-2)),
         ("GE large", scatter_e.large),
+        ("GE side", scatter_e.aside),
+        ("A mid", lambda: (strips_ae.middle(), strips_ar.middle())),
+        ("turn 2", lambda: turn(6, 2)),
         ("E finish", gather_e.finish),
         ("R step 1", lambda: gather_r.step(1)),
         ("E arrived", gather_e.arrived),
         ("hidden", hidden),
-        ("A mid", strips_a.middle),
         ("GE forward", scatter_e.forward),
-        ("load acts", loads[6].wait),
         ("GR tiles 0", lambda: gr_part(0, 4)),
+        ("GR tiles 1", lambda: gr_part(4, 2)),
+        ("GR tiles 2", lambda: gr_part(6, 2)),
         ("R step 2", lambda: gather_r.step(2)),
-        ("GR tiles 1", lambda: gr_part(4, 4)),
+        ("GR large", scatter_r.large),
         ("GE mid", scatter_e.middle),
-        ("GR large", scatter_r.large),
-        ("GE z", scatter_e.along_z),
+        ("GR side", scatter_r.aside),
         ("GR forward", scatter_r.forward),
         ("R step 3", lambda: gather_r.step(3)),
         ("GR mid", scatter_r.middle),
-        ("GE result", e_result),
+        ("GE z", scatter_e.along_z),
         ("GR z", scatter_r.along_z),
         ("R finish", gather_r.finish),
-        ("norm e", lambda: norm_step(norms_e, 0)),
+        ("GE result", lambda: result(0, scatter_e, norms_e, strips_ge)),
         ("R arrived", gather_r.arrived),
-        ("GR result", r_result),
-        ("A arrived", strips_a.arrived),
+        ("A arrived", lambda: (strips_ae.arrived(), strips_ar.arrived())),
+        ("GR result", lambda: result(1, scatter_r, norms_r, strips_gr)),
+        ("norm e", lambda: norm_step(norms_e)),
+        ("gE mid", strips_ge.middle),
         ("gi", lambda: lax.fori_loop(0, tiles, gi_tile, 0)),
-        ("E update", e_update),
-        ("norm r", lambda: norm_step(norms_r, 0)),
-        ("g mid", strips_g.middle),
-        ("NE mid", gather_ne.middle),
-        ("R update", r_update),
-        ("NE near 1", gather_ne.near_one),
-        ("NE fwd 0", lambda: gather_ne.forward(0)),
-        ("NE near 2", gather_ne.near_two),
+        ("norm r", lambda: norm_step(norms_r)),
+        ("gR mid", strips_gr.middle),
+        ("E update", lambda: update(0, ne, norms_e, strips_ge, gather_ne)),
+        ("R update", lambda: update(1, nr, norms_r, strips_gr, gather_nr)),
+        ("NE fwd 0", lambda: gather_ne.forward(0, -1, -3, -2)),
         ("NR fwd", lambda: gather_nr.forward(0, -1, -3, -2)),
-        ("NE fwd 1", lambda: gather_ne.forward(-1, -3, -2)),
+        ("NE finish", gather_ne.finish),
         ("NR finish", gather_nr.finish),
-        ("NE finish", gather_ne.finish),
+        ("NE arrived", gather_ne.arrived),
         ("NR arrived", gather_nr.arrived),
-        ("NE arrived", gather_ne.arrived),
     ]
     for name, step in program:
         with scope(name.replace(" ", "_")):
@@ -656,7 +659,7 @@
     with scope("drain"):
         for unit in (
             gather_e, gather_r, gather_ne, gather_nr, scatter_e, scatter_r,
-            strips_a, strips_g,
+            strips_ae, strips_ar, strips_ge, strips_gr,
         ):
             unit.unit.wait()
         norms_e.sent()
@@ -728,10 +731,11 @@
             pltpu.VMEM(whole, BF16),
             pltpu.VMEM((channels, middle), BF16),
             pltpu.VMEM((2, *own), F32),
-            pltpu.VMEM((NZ, BLK, middle), F32),
-            pltpu.VMEM((2, 4, NZ, BLK, half), F32),
-            pltpu.VMEM((NZ, BLK, middle), BF16),
-            pltpu.VMEM((2, 4, NZ, BLK, half), BF16),
+            pltpu.VMEM((2, NZ, BLK, middle), BF16),
+            pltpu.VMEM((2, 2, 4, NZ, BLK, half), BF16),
+            pltpu.VMEM((2, NZ, BLK, middle), BF16),
+            pltpu.VMEM((2, 2, 4, NZ, BLK, half), BF16),
+            pltpu.VMEM((channels, rows), BF16),
             scatter,
             scatter,
             norms,

time: 78.6 us -> 74.4 us (0.947)
  Pallas kernels: 77.8 us -> 73.6 us
    pallas_call x1, Pallas kernels: 75 us -> 70.7 us  [shards(): pl.pallas_call(kernel, out_shape=(pltpu.VMEM((rows, channels), BF16), plt...]
where the time goes in v5:
time: 74.4 us; the launch traced here: 74.2 us
  Pallas kernels  73.6 us (99%)
    pallas_call x1, Pallas kernels, shards(): pl.pallas_call(kernel, out_shape=(pltpu.VMEM((rows, channels), BF16), plt...  70.7 us
    pallas_call x1, Pallas kernels, shards(): pl.pallas_call(write_out, out_shape=(jax.ShapeDtypeStruct((rows, channels...  2.88 us

profile of v5, /device:TPU:1, one launch (start us, length us, event | category | flops | bytes accessed | tf_op | source)
XLA Modules:
  0.0 74.2 jit_solution(12814088752651926393)
XLA Ops:
  0.6 70.7 %shard_map.126 = (bf16[588,2048]{1,0:T(8,128)(2,1)S(1)}, f32[4,8,512]{2,1,0:T(8,128)S(1)}, bf16[8,4,8,8,512]{4,3,2,1,0:T(8,128)(2,1)S(1)}, bf16[8,4,8,8,512]{4,3,2,1,0:T(8,128)(2,1)S(1)}) custom-call(bf16[588,2048]{1,0:T(8,128)(2,1)} %acts_h.1, bf16[588,512]{1,0:T(8,128)(2,1)} %hid_h.1, bf16[588,2048]{1,0:T(8,128)(2,1)} %go_h.1, f32[8,512]{1,0:T(8,128)} %mr_h.1, ...), custom_call_target="tpu_custom_call" | custom-call | tf_op jit(solution)/shard_map/pallas_call | solution.py:713
  71.4 2.9 %shard_map.127 = (bf16[588,2048]{1,0:T(8,128)(2,1)}, f32[8,512]{1,0:T(8,128)}, f32[8,512]{1,0:T(8,128)}, f32[8,512]{1,0:T(8,128)}, f32[8,512]{1,0:T(8,128)}, /*i...) custom-call(bf16[588,2048]{1,0:T(8,128)(2,1)S(1)} %get-tuple-element.18.gi, ...), custom_call_target="tpu_custom_call" | custom-call | tf_op jit(solution)/shard_map/pallas_call | solution.py:752

commit v6 on v5

--- a/solution.py
+++ b/solution.py
@@ -11,6 +11,7 @@
 ROWS_SPLIT = ("gx", "gy", "gz")
 NZ, NY, NX, NK = 8, 4, 4, 2
 BLK = 8
+PIECES = 1
 FAR_FIRST = (4, 3, 5, 2, 6, 1, 7)
 STRIPS = (2, 1, 3, 0)
 PLANE = [(jy, jx) for jy in (2, 1, 3, 0) for jx in (2, 1, 3, 0)][:-1]
@@ -131,6 +132,10 @@
     def core(self, ref):
         self.put(ref, self.me.other(), self.cores)
 
+    def across(self, part, off):
+        me = self.me
+        return me.plane(0, 1, off + NX) if part == 0 else me.plane(off + NY, 1, 0)
+
     def near(self, part, mid):
         d = self.me.d
         self.ahead[part][mid] = self.net.group()
@@ -171,8 +176,10 @@
         for mid in mids:
             for part in range(2):
                 self.ahead[part][mid].wait()
-                group = self.far[part][0 if mid in (0, -1) else 1]
-                self.put(self.at(part, -d, mid), self.peer(part, d), group)
+                ref = self.at(part, -d, mid)
+                self.put(ref, self.peer(part, d), self.far[part][1 if mid == -2 else 0])
+                if mid == -2:
+                    self.put(ref, self.across(part, d), self.cores)
         if -2 in mids:
             for part in range(2):
                 self.core(self.slab(part, -d))
@@ -182,11 +189,12 @@
         for part in range(2):
             self.side[part].wait()
             self.core(self.slab(part, d))
-        for i, mids in enumerate(((0, -1), (-3, -2))):
-            for part in range(2):
-                self.far[part][i].wait()
-                for mid in mids:
-                    self.core(self.at(part, 2, mid))
+        for part in range(2):
+            self.far[part][0].wait()
+            for mid in (0, -1, -3):
+                self.core(self.at(part, 2, mid))
+        for part in range(2):
+            self.far[part][1].wait()
 
     def arrived(self):
         self.cores.wait()
@@ -339,9 +347,9 @@
                 self.joined(part, d, mid)
                 self.joined(part, 0, mid)
 
-    def forward(self):
+    def forward(self, *mids):
         d = self.me.d
-        for mid in STRIPS:
+        for mid in mids:
             for part in range(2):
                 self.near[part][mid].wait()
                 i = self.index(1 - part, mid)
@@ -351,10 +359,11 @@
                 dst = self.r.at[part, 1, i]
                 self.put(self.t.at[part, i], dst, self.peer(part, d), self.far[part][mid])
 
-    def middle(self):
-        for part in range(2):
-            self.side[part].wait()
-        for mid in STRIPS:
+    def middle(self, *mids):
+        if mids[0] == STRIPS[0]:
+            for part in range(2):
+                self.side[part].wait()
+        for mid in mids:
             for part in range(2):
                 self.far[part][mid].wait()
                 i = self.index(1 - part, mid)
@@ -615,38 +624,41 @@
         ("E fwd 2", lambda: gather_e.forward(-2)),
         ("GE large", scatter_e.large),
         ("GE side", scatter_e.aside),
-        ("A mid", lambda: (strips_ae.middle(), strips_ar.middle())),
         ("turn 2", lambda: turn(6, 2)),
         ("E finish", gather_e.finish),
         ("R step 1", lambda: gather_r.step(1)),
         ("E arrived", gather_e.arrived),
         ("hidden", hidden),
-        ("GE forward", scatter_e.forward),
+        ("GE forward", lambda: scatter_e.forward(*STRIPS)),
         ("GR tiles 0", lambda: gr_part(0, 4)),
         ("GR tiles 1", lambda: gr_part(4, 2)),
         ("GR tiles 2", lambda: gr_part(6, 2)),
         ("R step 2", lambda: gather_r.step(2)),
         ("GR large", scatter_r.large),
-        ("GE mid", scatter_e.middle),
+        ("GE mid", lambda: scatter_e.middle(*STRIPS)),
         ("GR side", scatter_r.aside),
-        ("GR forward", scatter_r.forward),
+        ("GR fwd 0", lambda: scatter_r.forward(2, 1)),
+        ("GR fwd 1", lambda: scatter_r.forward(3, 0)),
         ("R step 3", lambda: gather_r.step(3)),
-        ("GR mid", scatter_r.middle),
+        ("GR mid 0", lambda: scatter_r.middle(2, 1)),
         ("GE z", scatter_e.along_z),
+        ("GR mid 1", lambda: scatter_r.middle(3, 0)),
         ("GR z", scatter_r.along_z),
         ("R finish", gather_r.finish),
+        ("A mid", lambda: (strips_ae.middle(), strips_ar.middle())),
         ("GE result", lambda: result(0, scatter_e, norms_e, strips_ge)),
-        ("R arrived", gather_r.arrived),
-        ("A arrived", lambda: (strips_ae.arrived(), strips_ar.arrived())),
         ("GR result", lambda: result(1, scatter_r, norms_r, strips_gr)),
         ("norm e", lambda: norm_step(norms_e)),
         ("gE mid", strips_ge.middle),
-        ("gi", lambda: lax.fori_loop(0, tiles, gi_tile, 0)),
+        ("R arrived", gather_r.arrived),
+        ("gi", lambda: lax.fori_loop(0, tiles, gi_tile, 0, unroll=2)),
+        ("A arrived", lambda: (strips_ae.arrived(), strips_ar.arrived())),
         ("norm r", lambda: norm_step(norms_r)),
         ("gR mid", strips_gr.middle),
         ("E update", lambda: update(0, ne, norms_e, strips_ge, gather_ne)),
         ("R update", lambda: update(1, nr, norms_r, strips_gr, gather_nr)),
-        ("NE fwd 0", lambda: gather_ne.forward(0, -1, -3, -2)),
+        ("NE fwd 0", lambda: gather_ne.forward(0, -1)),
+        ("NE fwd 1", lambda: gather_ne.forward(-3, -2)),
         ("NR fwd", lambda: gather_nr.forward(0, -1, -3, -2)),
         ("NE finish", gather_ne.finish),
         ("NR finish", gather_nr.finish),
@@ -668,20 +680,14 @@
 
 
 def write_out(gi, small, ne, nr, gi_h, nmr_h, nme_h, nvr_h, nve_h, wr_h, we_h, sem):
-    copies = [
-        pltpu.make_async_copy(src, dst, sem.at[i])
-        for i, (src, dst) in enumerate(
-            (
-                (gi, gi_h),
-                (ne, we_h),
-                (nr, wr_h),
-                (small.at[0], nme_h),
-                (small.at[1], nve_h),
-                (small.at[2], nmr_h),
-                (small.at[3], nvr_h),
-            )
-        )
-    ]
+    pairs = [(small.at[i], ref) for i, ref in enumerate((nme_h, nve_h, nmr_h, nvr_h))]
+    for i in range(PIECES):
+        zs = pl.ds(i * (NZ // PIECES), NZ // PIECES)
+        wide = gi.shape[1] // PIECES
+        cols = pl.ds(i * wide, wide)
+        pairs += [(nr.at[zs], wr_h.at[zs]), (ne.at[zs], we_h.at[zs])]
+        pairs += [(gi.at[:, cols], gi_h.at[:, cols])]
+    copies = [pltpu.make_async_copy(src, dst, sem.at[i]) for i, (src, dst) in enumerate(pairs)]
     for copy in copies:
         copy.start()
     for copy in copies:
@@ -762,7 +768,7 @@
         ),
         in_specs=[vmem] * 4,
         out_specs=(in_hbm,) * 7,
-        scratch_shapes=[pltpu.SemaphoreType.DMA((7,))],
+        scratch_shapes=[pltpu.SemaphoreType.DMA((4 + 3 * PIECES,))],
         compiler_params=pltpu.CompilerParams(vmem_limit_bytes=4 * 1024 * 1024),
     )(*results)
     flat = (channels, middle)

time: 74.4 us -> 72.7 us (0.977)
  Pallas kernels: 73.6 us -> 71.9 us
    pallas_call x1, Pallas kernels: 70.7 us -> 69 us  [shards(): pl.pallas_call(kernel, out_shape=(pltpu.VMEM((rows, channels), BF16), plt...]
where the time goes in v6:
time: 72.7 us; the launch traced here: 72.5 us
  Pallas kernels  71.9 us (99%)
    pallas_call x1, Pallas kernels, shards(): pl.pallas_call(kernel, out_shape=(pltpu.VMEM((rows, channels), BF16), plt...  69 us
    pallas_call x1, Pallas kernels, shards(): pl.pallas_call(write_out, out_shape=(jax.ShapeDtypeStruct((rows, channels...  2.89 us

profile of v6, /device:TPU:1, one launch (start us, length us, event | category | flops | bytes accessed | tf_op | source)
XLA Modules:
  0.0 72.5 jit_solution(9744846223057255837)
XLA Ops:
  0.6 69.0 %shard_map.126 = (bf16[588,2048]{1,0:T(8,128)(2,1)S(1)}, f32[4,8,512]{2,1,0:T(8,128)S(1)}, bf16[8,4,8,8,512]{4,3,2,1,0:T(8,128)(2,1)S(1)}, bf16[8,4,8,8,512]{4,3,2,1,0:T(8,128)(2,1)S(1)}) custom-call(bf16[588,2048]{1,0:T(8,128)(2,1)} %acts_h.1, bf16[588,512]{1,0:T(8,128)(2,1)} %hid_h.1, bf16[588,2048]{1,0:T(8,128)(2,1)} %go_h.1, f32[8,512]{1,0:T(8,128)} %mr_h.1, ...), custom_call_target="tpu_custom_call" | custom-call | tf_op jit(solution)/shard_map/pallas_call | solution.py:719
  69.6 2.9 %shard_map.127 = (bf16[588,2048]{1,0:T(8,128)(2,1)}, f32[8,512]{1,0:T(8,128)}, f32[8,512]{1,0:T(8,128)}, f32[8,512]{1,0:T(8,128)}, f32[8,512]{1,0:T(8,128)}, /*i...) custom-call(bf16[588,2048]{1,0:T(8,128)(2,1)S(1)} %get-tuple-element.18.gi, ...), custom_call_target="tpu_custom_call" | custom-call | tf_op jit(solution)/shard_map/pallas_call | solution.py:758
